TPU v7x, 32 devices: a whole 2x2x4 slice. The times are simulated.
32 devices in a mesh: seq: 8 (over y, x, core), tp: 4 (over z).
Axes of the slice: x: 2, y: 2, z: 4, core: 2. Of those that a mesh axis runs over, the one named last changes fastest.
Arguments:
- states: bfloat16 [8, 128, 2048], P('seq', None, 'tp'), may hold values from -60 to 60, as said below
- cotangent: bfloat16 [8, 128, 2048], P('seq', None, 'tp'), may hold values from -12 to 12, as said below
- wq: bfloat16 [2048, 2048], P(None, 'tp'), may hold values from -0.125 to 0.125
- wk: bfloat16 [2048, 512], P(None, 'tp'), may hold values from -0.125 to 0.125
- wv: bfloat16 [2048, 512], P(None, 'tp'), may hold values from -0.125 to 0.125
- wo: bfloat16 [2048, 2048], P('tp'), may hold values from -0.125 to 0.125
Outputs:
- gram: float32 [8, 8], P('seq')
Inputs may be any that keep to these rules, and one draw needn't show every extreme that they name: `states`: finite values. `cotangent`: finite values.
All inputs are finite; a program needn't handle non-finite values.
Results may differ from a plain program's by a relative error of at most 0.0025.
Values may be sent and summed in bfloat16 or wider, within the bound.
A program may use at most 64 MiB of HBM per device.

v0:
```python
import functools

import jax
import jax.numpy as jnp
import numpy as np
from jax import lax
from jax.experimental import pallas as pl
from jax.experimental.pallas import tpu as pltpu
from jax.sharding import PartitionSpec as P

HEADS = 32
KV_HEADS = 8
HEAD_DIM = 64
THETA = 500000.0
LANES = 128
GROUP = HEADS // KV_HEADS
F32, BF16 = jnp.float32, jnp.bfloat16

NT = (((1,), (1,)), ((), ()))
TN = (((0,), (0,)), ((), ()))


def rope_tables(length):
    half = HEAD_DIM // 2
    freqs = np.float32(THETA) ** (-(np.arange(half, dtype=np.float32) * np.float32(2.0 / HEAD_DIM)))
    angles = np.arange(length, dtype=np.float32)[:, None] * freqs[None, :].astype(np.float32)
    cos, sin = np.cos(angles), np.sin(angles)
    return (
        np.concatenate([cos, cos] * 2, axis=1).astype(np.float32),
        np.concatenate([-sin, sin] * 2, axis=1).astype(np.float32),
    )


def dot(a, b, dims=None):
    if dims is None:
        return jnp.dot(a, b, preferred_element_type=F32)
    return lax.dot_general(a, b, dims, preferred_element_type=F32)


def place_of(index, n):
    if n % 8:
        return index
    block, rest = index // 8, index % 8
    row, col, core = rest // 4, (rest // 2) % 2, rest % 2
    return block * 8 + 2 * (2 * row + (row + col) % 2) + core


def index_at(place, n):
    if n % 8:
        return place
    block, rest = place // 8, place % 8
    spot, core = rest // 2, rest % 2
    row = spot // 2
    return block * 8 + 2 * (2 * row + (row + spot) % 2) + core


def kernel(
    n, tp,
    states_ref, cot_ref, cos_ref, sin_ref, wq_hbm, wk_hbm, wv_hbm, wo_hbm,
    out_ref,
    xs, cs, wqb, wkb, wvb, wob, q_acc, k_acc, v_acc, g_acc,
    fs, fc, att_own, att_in, gv_own, gv_in, probs, ad, rs, full, t2,
    w_sem, x_snd, x_rcv, p_snd, p_rcv, a_snd, a_rcv, g_snd, g_rcv,
    rs_snd, rs_rcv, ag_snd, ag_rcv, r2_snd, r2_rcv,
):
    length, width = states_ref.shape
    kv_cols = k_acc.shape[1]
    half = n // 2
    rows = length // tp
    lanes = t2.shape[3]
    me = lax.axis_index("seq")
    col = lax.axis_index("tp")
    place = place_of(me, n)

    def turn(d):
        return d * (1 - 2 * ((d + 1) % 2))

    def source(d):
        return index_at((place + turn(d) + n) % n, n)

    def target(d):
        return index_at((place - turn(d) + n) % n, n)

    def peer(k):
        return (col + k) % tp

    def each(lo, hi, body):
        if hi - lo <= 8:
            for i in range(lo, hi):
                body(i)
        else:
            lax.fori_loop(lo, hi, lambda i, c: (body(i), c)[1], 0)

    weight_copies = []
    for k in range(tp):
        at = pl.ds(pl.multiple_of(((col - k + tp) % tp) * width, width), width)
        copies = [
            pltpu.make_async_copy(wq_hbm.at[at, :], wqb.at[k], w_sem.at[4 * k]),
            pltpu.make_async_copy(wk_hbm.at[at, :], wkb.at[k], w_sem.at[4 * k + 1]),
            pltpu.make_async_copy(wv_hbm.at[at, :], wvb.at[k], w_sem.at[4 * k + 2]),
            pltpu.make_async_copy(wo_hbm.at[:, at], wob.at[k], w_sem.at[4 * k + 3]),
        ]
        weight_copies.append(copies)

    barrier = pltpu.get_barrier_semaphore()
    for k in range(1, tp):
        pl.semaphore_signal(barrier, inc=1, device_id={"tp": peer(k)})
    each(1, n, lambda o: pl.semaphore_signal(barrier, inc=1, device_id={"seq": (me + o) % n}))
    for copies in weight_copies:
        for c in copies:
            c.start()
    pl.semaphore_wait(barrier, tp - 1 + n - 1)

    def remote(src, dst, snd, rcv, device):
        return pltpu.make_async_remote_copy(
            src_ref=src, dst_ref=dst, send_sem=snd, recv_sem=rcv, device_id=device
        )

    inputs = (states_ref, cot_ref)
    held = (xs, cs)

    def up(which, k):
        src = inputs[which] if k == 1 else held[which].at[k - 2]
        return remote(
            src, held[which].at[k - 1], x_snd.at[which, 0, k - 1], x_rcv.at[which, k - 1],
            {"tp": peer(1)},
        )

    def down(which, k):
        src = inputs[which] if k == 1 else held[which].at[tp - k]
        return remote(
            src, held[which].at[tp - k - 1], x_snd.at[which, 1, k - 1],
            x_rcv.at[which, tp - k - 1], {"tp": peer(tp - 1)},
        )

    def sends_up(k):
        return (col >= k - 1) & (col < tp - 1)

    def sends_down(k):
        return (col + k - 1 < tp) & (col > 0)

    def pass_on(which, k, act):
        @pl.when(sends_up(k))
        def _():
            act(up(which, k))

        @pl.when(sends_down(k))
        def _():
            act(down(which, k))

    def arrivals(k, body):
        pl.when(col >= k)(lambda: body(k))
        pl.when(col + k < tp)(lambda: body(tp - k))

    def await_block(which, k):
        arrivals(
            k,
            lambda slot: remote(
                inputs[which], held[which].at[slot - 1], x_snd.at[which, 0, 0],
                x_rcv.at[which, slot - 1], {"tp": peer(1)},
            ).wait_recv(),
        )

    for which in range(2):
        pass_on(which, 1, lambda c: c.start())

    def plane_copies(d):
        to = {"seq": target(d)}
        return (
            remote(states_ref, fs.at[d - 1], p_snd.at[0, d - 1], p_rcv.at[0, d - 1], to),
            remote(cot_ref, fc.at[d - 1], p_snd.at[1, d - 1], p_rcv.at[1, d - 1], to),
        )

    def start_plane(d):
        for c in plane_copies(d):
            c.start()

    each(1, half + 1, start_plane)

    def project_states(slot):
        for c in weight_copies[slot][:3]:
            c.wait()
        x = states_ref[...] if slot == 0 else xs[slot - 1]
        for acc, w in ((q_acc, wqb), (k_acc, wkb), (v_acc, wvb)):
            piece = dot(x, w[slot])
            acc[...] = piece if slot == 0 else acc[...] + piece

    def project_cot(slot):
        weight_copies[slot][3].wait()
        y = cot_ref[...] if slot == 0 else cs[slot - 1]
        piece = dot(y, wob[slot], NT)
        g_acc[...] = piece if slot == 0 else g_acc[...] + piece

    lane = lax.broadcasted_iota(jnp.int32, (length, LANES), 1)
    low = lane < HEAD_DIM
    first = lane % HEAD_DIM < HEAD_DIM // 2
    cos, sin = cos_ref[...], sin_ref[...]
    causal = lax.broadcasted_iota(jnp.int32, (length, length), 0) >= lax.broadcasted_iota(
        jnp.int32, (length, length), 1
    )

    def swap(v):
        return pltpu.roll(v, HEAD_DIM, 1)

    def rope(v):
        turned = jnp.where(
            first, pltpu.roll(v, LANES - HEAD_DIM // 2, 1), pltpu.roll(v, HEAD_DIM // 2, 1)
        )
        return v * cos + turned * sin

    def halves(v):
        other = swap(v)
        zero = jnp.zeros_like(v)
        return (
            (jnp.where(low, v, zero).astype(BF16), jnp.where(low, zero, other).astype(BF16)),
            (jnp.where(low, other, zero).astype(BF16), jnp.where(low, zero, v).astype(BF16)),
        )

    blocks = [
        (b, g, (b * 2 + g) * (GROUP // 2) + pair)
        for b in range(kv_cols // LANES)
        for g in range(2)
        for pair in range(GROUP // 2)
    ]

    part_cols = width // 2

    def attend(part):
        share = len(blocks) // 2
        for b, g, at in blocks[part * share : (part + 1) * share]:
            kcut, cut = slice(b * LANES, (b + 1) * LANES), slice(at * LANES, (at + 1) * LANES)
            keys = halves(rope(k_acc[:, kcut]))
            values = halves(v_acc[:, kcut])
            q = rope(q_acc[:, cut]).astype(BF16)
            att = None
            for side in range(2):
                s = dot(q, keys[g][side], NT) * HEAD_DIM ** (-0.5)
                s = jnp.where(causal, s, -jnp.inf)
                e = jnp.exp(s - jnp.max(s, axis=1, keepdims=True))
                p = (e / jnp.sum(e, axis=1, keepdims=True)).astype(BF16)
                probs[2 * at + side] = p
                a = dot(p, values[g][side])
                att = a if att is None else att + a
            att_own[:, cut] = att.astype(BF16)

    def grad_values():
        sums = {}
        for b, g, at in blocks:
            ga = g_acc[:, at * LANES : (at + 1) * LANES].astype(BF16)
            for side in range(2):
                u = dot(probs[2 * at + side], ga, TN)
                key = (b, g, side)
                sums[key] = sums[key] + u if key in sums else u
        for b in range(kv_cols // LANES):
            grad = jnp.where(
                low,
                sums[b, 0, 0] + swap(sums[b, 0, 1]),
                swap(sums[b, 1, 0]) + sums[b, 1, 1],
            )
            gv_own[:, b * LANES : (b + 1) * LANES] = grad.astype(BF16)

    def att_copy(d, part):
        cut = pl.ds(part * part_cols, part_cols)
        return remote(
            att_own.at[:, cut], att_in.at[d - 1, :, cut], a_snd.at[part, d - 1],
            a_rcv.at[part, d - 1], {"seq": target(d)},
        )

    def gv_copy(d):
        return remote(
            gv_own, gv_in.at[d - 1], g_snd.at[d - 1], g_rcv.at[d - 1], {"seq": target(d)}
        )

    def band(k):
        return pl.ds(pl.multiple_of(k * rows, rows), rows)

    def rs_copies(d):
        two = pl.ds(2 * d, 2)
        return [
            remote(
                ad.at[two, band(peer(k)), :], rs.at[k - 1, two], rs_snd.at[k - 1, d],
                rs_rcv.at[k - 1, d], {"tp": peer(k)},
            )
            for k in range(1, tp)
        ]

    def ag_copies(d):
        part = full.at[pl.ds(2 * d, 2), band(col), :]
        return [
            remote(part, part, ag_snd.at[k - 1, d], ag_rcv.at[k - 1, d], {"tp": peer(k)})
            for k in range(1, tp)
        ]

    def multiply(d, states_other, cot_other):
        ad[2 * d] = dot(states_ref[...], states_other[...], NT).astype(BF16)
        ad[2 * d + 1] = dot(cot_ref[...], cot_other[...], NT).astype(BF16)
        for c in rs_copies(d):
            c.start()

    def pair(d):
        for c in plane_copies(d):
            c.wait_recv()
        multiply(d, fs.at[d - 1], fc.at[d - 1])

    def gather_sum(d):
        for c in rs_copies(d):
            c.wait_recv()
        two = pl.ds(2 * d, 2)
        total = ad[two, band(col), :].astype(F32)
        for k in range(1, tp):
            total = total + rs[k - 1, two].astype(F32)
        full[two, band(col), :] = total.astype(BF16)
        for c in ag_copies(d):
            c.start()

    bounds = [1 + (half * k + tp - 2) // (tp - 1) for k in range(tp)]

    project_states(0)
    multiply(0, states_ref, cot_ref)
    project_cot(0)
    for k in range(1, tp):
        last = k == tp - 1
        await_block(0, k)
        if not last:
            pass_on(0, k + 1, lambda c: c.start())
        arrivals(k, project_states)
        if last:
            each(bounds[k - 1], bounds[k], pair)
            for part in range(2):
                attend(part)
                each(1, half + 1, lambda d: att_copy(d, part).start())
            each(bounds[k - 2] if k > 1 else 0, bounds[k], gather_sum)
        await_block(1, k)
        if not last:
            pass_on(1, k + 1, lambda c: c.start())
        arrivals(k, project_cot)
        if not last:
            each(bounds[k - 1], bounds[k], pair)
            each(bounds[k - 2] if k > 1 else 0, bounds[k - 1], gather_sum)
    grad_values()
    each(1, half + 1, lambda d: gv_copy(d).start())

    lane_at = lax.broadcasted_iota(jnp.int32, (1, lanes), 1)

    def entry(d, att_other, gv_other):
        b = dot(gv_own[...], gv_other[...], NT)
        c = dot(att_own[...], att_other[...], NT)
        product = full[2 * d].astype(F32) * b + full[2 * d + 1].astype(F32) * c
        return jnp.sum(jnp.sum(product, axis=0, keepdims=True), axis=1, keepdims=True)

    def settle(d):
        for c in ag_copies(d):
            c.wait_recv()

    settle(0)
    t2[col, me] = jnp.where(lane_at == me, entry(0, att_own, gv_own), 0.0)

    def score(d):
        settle(d)
        for part in range(2):
            att_copy(d, part).wait_recv()
        gv_copy(d).wait_recv()
        value = entry(d, att_in.at[d - 1], gv_in.at[d - 1])
        t2[col, me] += jnp.where(lane_at == source(d), value, 0.0)

    each(1, half + 1, score)

    def r2_copy(o):
        mine = t2.at[col, me]
        to = {"seq": (me + o) % n, "tp": (col + o // n) % tp}
        return remote(mine, mine, r2_snd.at[o - 1], r2_rcv.at[o - 1], to)

    def every(act):
        if n * tp <= 32:
            for o in range(1, n * tp):
                act(r2_copy(o))
        else:
            each(1, n * tp, lambda o: act(r2_copy(o)))

    every(lambda c: c.start())
    every(lambda c: c.wait_recv())

    table = t2[0].reshape(n, lanes)
    for q in range(1, tp):
        table = table + t2[q].reshape(n, lanes)
    rank = lax.broadcasted_iota(jnp.int32, (n, lanes), 0)
    spot = lax.broadcasted_iota(jnp.int32, (n, lanes), 1)
    eye = rank == spot
    column = jnp.sum(jnp.where(spot == me, table, 0.0), axis=1, keepdims=True)
    theirs = eye & (rank != me) & (rank != source(half))
    mirrored = jnp.sum(jnp.where(theirs, column, 0.0), axis=0, keepdims=True)
    own = jnp.sum(jnp.where(rank == me, table, 0.0), axis=0, keepdims=True)
    diag = jnp.sum(jnp.where(eye, table, 0.0), axis=0, keepdims=True)
    own_diag = jnp.sum(jnp.where(lane_at == me, diag, 0.0), axis=1, keepdims=True)
    gram = (own + mirrored) / jnp.sqrt(own_diag * diag)
    out_ref[...] = gram[:, :n]

    for k in range(1, tp):
        for which in range(2):
            pass_on(which, k, lambda c: c.wait_send())

    def drain_sums(d):
        for c in rs_copies(d) + ag_copies(d):
            c.wait_send()

    each(0, half + 1, drain_sums)

    def drain(d):
        for c in plane_copies(d):
            c.wait_send()
        for part in range(2):
            att_copy(d, part).wait_send()
        gv_copy(d).wait_send()

    each(1, half + 1, drain)
    every(lambda c: c.wait_send())


def on_device(n, tp, states, cotangent, wq, wk, wv, wo):
    seq_dev, length, width = states.shape
    assert seq_dev == 1 and n % 2 == 0 and length == LANES
    kv = wk.shape[1]
    half = n // 2
    tiles = 2 * (half + 1)
    lanes = -(-n // LANES) * LANES
    cos, sin = rope_tables(length)
    vmem = pl.BlockSpec(memory_space=pltpu.VMEM)
    hbm = pl.BlockSpec(memory_space=pl.ANY)
    sem = pltpu.SemaphoreType.DMA
    return pl.pallas_call(
        functools.partial(kernel, n, tp),
        out_shape=jax.ShapeDtypeStruct((1, n), F32),
        in_specs=[vmem] * 4 + [hbm] * 4,
        out_specs=vmem,
        scratch_shapes=[
            pltpu.VMEM((tp - 1, length, width), BF16),
            pltpu.VMEM((tp - 1, length, width), BF16),
            pltpu.VMEM((tp, width, wq.shape[1]), BF16),
            pltpu.VMEM((tp, width, kv), BF16),
            pltpu.VMEM((tp, width, kv), BF16),
            pltpu.VMEM((tp, wo.shape[0], width), BF16),
            pltpu.VMEM((length, wq.shape[1]), F32),
            pltpu.VMEM((length, kv), F32),
            pltpu.VMEM((length, kv), F32),
            pltpu.VMEM((length, wo.shape[0]), F32),
            pltpu.VMEM((half, length, width), BF16),
            pltpu.VMEM((half, length, width), BF16),
            pltpu.VMEM((length, width), BF16),
            pltpu.VMEM((half, length, width), BF16),
            pltpu.VMEM((length, kv), BF16),
            pltpu.VMEM((half, length, kv), BF16),
            pltpu.VMEM((width // HEAD_DIM, length, length), BF16),
            pltpu.VMEM((tiles, length, length), BF16),
            pltpu.VMEM((tp - 1, tiles, length // tp, length), BF16),
            pltpu.VMEM((tiles, length, length), BF16),
            pltpu.VMEM((tp, n, 1, lanes), F32),
            sem((4 * tp,)),
            sem((2, 2, tp - 1)),
            sem((2, tp - 1)),
            sem((2, half)),
            sem((2, half)),
            sem((2, half)),
            sem((2, half)),
            sem((half,)),
            sem((half,)),
            sem((tp - 1, half + 1)),
            sem((tp - 1, half + 1)),
            sem((tp - 1, half + 1)),
            sem((tp - 1, half + 1)),
            sem((n * tp - 1,)),
            sem((n * tp - 1,)),
        ],
        compiler_params=pltpu.CompilerParams(
            collective_id=0, has_side_effects=True, vmem_limit_bytes=60 * 1024 * 1024
        ),
        name="ntk_gram",
    )(
        states.reshape(length, width), cotangent.reshape(length, width),
        jnp.asarray(cos), jnp.asarray(sin), wq, wk, wv, wo,
    )


def solution(mesh):
    in_specs = (
        P("seq", None, "tp"),
        P("seq", None, "tp"),
        P(None, "tp"),
        P(None, "tp"),
        P(None, "tp"),
        P("tp", None),
    )
    return jax.shard_map(
        functools.partial(on_device, mesh.shape["seq"], mesh.shape["tp"]),
        mesh=mesh, in_specs=in_specs, out_specs=P("seq", None), check_vma=False,
    )
```

profile of v0, /device:TPU:0, one launch (start us, length us, event | category | flops | bytes accessed | tf_op | source)
XLA Modules:
  0.0 47.9 jit_solution(10302723042549222579)
XLA Ops:
  0.0 46.7 %ntk_gram.1 = f32[1,8]{1,0:T(1,128)} custom-call(bf16[128,512]{1,0:T(8,128)(2,1)} %bitcast.2, bf16[128,512]{1,0:T(8,128)(2,1)} %bitcast.3, f32[128,128]{1,0:T(8,128)} %constant.4.clone.cos_ref, f32[128,128]{1,0:T(8,128)} %constant.5.clone.sin_ref, bf16[2048,512]{1,0:T(8,128)(2,1)} %wq_hbm.1, bf16[2048,128]{1,0:T(8,128)(2,1)} %wk_hbm.1, ...), custom_call_target="tpu_custom_call" | custom-call | tf_op jit(solution)/shard_map/ntk_gram/pallas_call | solution.py:430
  46.7 1.2 %copy.10 = f32[1,8]{1,0:T(1,128)} copy(f32[1,8]{1,0:T(1,128)} %ntk_gram.1) | data formatting | bytes 64
where the time goes:
time: 48.1 us; the launch traced here: 47.9 us
  Pallas kernels  46.7 us (97%)
  local copies, waits for them, and re-layouts  1.19 us (2%)
    pallas_call x1, Pallas kernels, on_device(): pl.pallas_call(functools.partial(kernel, n, tp), out_shape=jax.ShapeDtype...  46.7 us
    unnamed x1, local copies, waits for them, and re-layouts  1.19 us

commit v1 on v0

v1 whole, which is shorter than its diff:
```python
import functools

import jax
import jax.numpy as jnp
import numpy as np
from jax import lax
from jax.experimental import pallas as pl
from jax.experimental.pallas import tpu as pltpu
from jax.sharding import PartitionSpec as P

HEADS = 32
KV_HEADS = 8
HEAD_DIM = 64
THETA = 500000.0
LANES = 128
HALVES = 2
GROUP = HEADS // KV_HEADS
F32, BF16 = jnp.float32, jnp.bfloat16

NT = (((1,), (1,)), ((), ()))
TN = (((0,), (0,)), ((), ()))


def rope_tables(length):
    half = HEAD_DIM // 2
    freqs = np.float32(THETA) ** (-(np.arange(half, dtype=np.float32) * np.float32(2.0 / HEAD_DIM)))
    angles = np.arange(length, dtype=np.float32)[:, None] * freqs[None, :].astype(np.float32)
    cos, sin = np.cos(angles), np.sin(angles)
    return (
        np.concatenate([cos, cos] * 2, axis=1).astype(np.float32),
        np.concatenate([-sin, sin] * 2, axis=1).astype(np.float32),
    )


def dot(a, b, dims=None):
    if dims is None:
        return jnp.dot(a, b, preferred_element_type=F32)
    return lax.dot_general(a, b, dims, preferred_element_type=F32)


def place_of(index, n):
    if n % 8:
        return index
    block, rest = index // 8, index % 8
    row, col, core = rest // 4, (rest // 2) % 2, rest % 2
    return block * 8 + 2 * (2 * row + (row + col) % 2) + core


def index_at(place, n):
    if n % 8:
        return place
    block, rest = place // 8, place % 8
    spot, core = rest // 2, rest % 2
    row = spot // 2
    return block * 8 + 2 * (2 * row + (row + spot) % 2) + core


def kernel(
    n, tp,
    states_ref, cot_ref, cos_ref, sin_ref, wq_hbm, wk_hbm, wv_hbm, wo_hbm,
    out_ref,
    xs, cs, wqb, wkb, wvb, wob, q_acc, k_acc, v_acc, g_acc,
    x_in, c_in, d_in, b_in, att_own, a_in, ad_in, ab_in, gv_own, g_in, gd_in, gb_in,
    probs, ad, rin, xin, full, t2,
    w_sem, z_snd, z_rcv, p_snd, p_rcv, f_snd, f_rcv, b_snd, b_rcv,
    a_snd, a_rcv, af_snd, af_rcv, g_snd, g_rcv,
    i_snd, r_rcv, s_rcv, o_snd, o_rcv, r2_snd, r2_rcv,
):
    length, width = states_ref.shape
    kv_cols = k_acc.shape[1]
    ring = n // 2
    far = ring // 2
    mid = tp // 2
    hrows = length // HALVES
    lanes = t2.shape[3]
    me = lax.axis_index("seq")
    col = lax.axis_index("tp")
    place = place_of(me, n)
    chip, core = place // 2, place % 2
    low_chip = chip < far
    last = tp - 1

    def device(hop, c):
        return index_at(2 * ((chip + hop + ring) % ring) + c, n)

    partner = device(0, 1 - core)

    def each(lo, hi, body):
        if hi - lo <= 8:
            for i in range(lo, hi):
                body(i)
        else:
            lax.fori_loop(lo, hi, lambda i, c: (body(i), c)[1], 0)

    def remote(src, dst, snd, rcv, to):
        return pltpu.make_async_remote_copy(
            src_ref=src, dst_ref=dst, send_sem=snd, recv_sem=rcv, device_id=to
        )

    weight_copies = []
    for k in range(tp):
        at = pl.ds(pl.multiple_of(((col - k + tp) % tp) * width, width), width)
        weight_copies.append([
            pltpu.make_async_copy(wq_hbm.at[at, :], wqb.at[k], w_sem.at[4 * k]),
            pltpu.make_async_copy(wk_hbm.at[at, :], wkb.at[k], w_sem.at[4 * k + 1]),
            pltpu.make_async_copy(wv_hbm.at[at, :], wvb.at[k], w_sem.at[4 * k + 2]),
            pltpu.make_async_copy(wo_hbm.at[:, at], wob.at[k], w_sem.at[4 * k + 3]),
        ])

    barrier = pltpu.get_barrier_semaphore()
    pl.when(col > 0)(
        lambda: pl.semaphore_signal(barrier, inc=1, device_id={"tp": col - 1})
    )
    pl.when(col < last)(
        lambda: pl.semaphore_signal(barrier, inc=1, device_id={"tp": col + 1})
    )
    each(1, n, lambda o: pl.semaphore_signal(barrier, inc=1, device_id={"seq": (me + o) % n}))
    order = [0] + [s for k in range(1, tp) for s in dict.fromkeys((k, tp - k)) if k <= tp - k]
    for part in (slice(0, 3), slice(3, 4)):
        for k in order:
            for c in weight_copies[k][part]:
                c.start()
    ends = (col == 0).astype(jnp.int32) + (col == last).astype(jnp.int32)
    pl.semaphore_wait(barrier, n + 1 - ends)

    inputs = (states_ref, cot_ref)
    held = (xs, cs)

    def rows_of(h):
        return pl.ds(h * hrows, hrows)

    def up(which, k, h):
        src = inputs[which] if k == 1 else held[which].at[k - 2]
        return remote(
            src.at[rows_of(h), :], held[which].at[k - 1, rows_of(h), :],
            z_snd.at[which, 0, k - 1, h], z_rcv.at[which, k - 1, h], {"tp": (col + 1) % tp},
        )

    def down(which, k, h):
        src = inputs[which] if k == 1 else held[which].at[tp - k]
        return remote(
            src.at[rows_of(h), :], held[which].at[tp - k - 1, rows_of(h), :],
            z_snd.at[which, 1, k - 1, h], z_rcv.at[which, tp - k - 1, h],
            {"tp": (col + tp - 1) % tp},
        )

    def sends_up(k):
        return (col >= k - 1) & (col < last)

    def sends_down(k):
        return (col + k - 1 < tp) & (col > 0)

    def landed(which, slot, h):
        remote(
            inputs[which].at[rows_of(h), :], held[which].at[slot - 1, rows_of(h), :],
            z_snd.at[which, 0, 0, h], z_rcv.at[which, slot - 1, h], {"tp": (col + 1) % tp},
        ).wait_recv()

    def begin_up(which):
        for h in range(HALVES):
            up(which, 1, h).start()

    def begin_down(which):
        for h in range(HALVES):
            down(which, 1, h).start()

    def relay(which, k):
        for h in range(HALVES):
            @pl.when((col >= k) & (col < last))
            def _():
                landed(which, k, h)
                up(which, k + 1, h).start()

            @pl.when((col + k < tp) & (col > 0))
            def _():
                landed(which, tp - k, h)
                down(which, k + 1, h).start()

    def settle(which, k):
        for h in range(HALVES):
            pl.when((col >= k) & (col == last))(lambda: landed(which, k, h))
            pl.when((col + k < tp) & (col == 0))(lambda: landed(which, tp - k, h))

    def arrivals(k, body):
        pl.when(col >= k)(lambda: body(k))
        pl.when(col + k < tp)(lambda: body(tp - k))

    def follow(k):
        pl.when((col == k) & (col < last))(lambda: begin_up(1))
        pl.when((last - col == k) & (col > 0))(lambda: begin_down(1))

    pl.when(col < last)(lambda: begin_up(0))
    pl.when(col > 0)(lambda: begin_down(0))
    follow(0)

    def x_copy(d):
        return remote(
            states_ref, x_in.at[2 * (d - 1)], p_snd.at[0, d - 1], p_rcv.at[0, d - 1],
            {"seq": device(-d, core)},
        )

    def c_copy(d):
        return remote(
            cot_ref, c_in.at[2 * (d - 1)], p_snd.at[1, d - 1], p_rcv.at[1, d - 1],
            {"seq": device(d, core)},
        )

    def far_copy(src):
        return remote(
            src, d_in.at[0], p_snd.at[2, 0], p_rcv.at[2, 0], {"seq": device(far, core)}
        )

    def beside_copy(src):
        return remote(src, b_in, b_snd.at[0], b_rcv.at[0], {"seq": partner})

    def x_pass(d):
        return remote(
            x_in.at[2 * (d - 1)], x_in.at[2 * (d - 1) + 1], f_snd.at[0, d - 1],
            f_rcv.at[0, d - 1], {"seq": partner},
        )

    def c_pass(d):
        return remote(
            c_in.at[2 * (d - 1)], c_in.at[2 * (d - 1) + 1], f_snd.at[1, d - 1],
            f_rcv.at[1, d - 1], {"seq": partner},
        )

    def far_pass():
        return remote(
            d_in.at[0], d_in.at[1], f_snd.at[2, 0], f_rcv.at[2, 0], {"seq": partner}
        )

    def start_near(d):
        x_copy(d).start()
        c_copy(d).start()

    pl.when(core == 1)(lambda: beside_copy(states_ref).start())
    pl.when(core == 0)(lambda: beside_copy(cot_ref).start())
    each(1, far, start_near)
    pl.when(low_chip)(lambda: far_copy(states_ref).start())
    pl.when(chip >= far)(lambda: far_copy(cot_ref).start())

    def pass_near(d):
        x_copy(d).wait_recv()
        x_pass(d).start()
        c_copy(d).wait_recv()
        c_pass(d).start()

    def pass_far():
        far_copy(states_ref).wait_recv()
        far_pass().start()

    def project_states(slot):
        for c in weight_copies[slot][:3]:
            c.wait()
        x = states_ref[...] if slot == 0 else xs[slot - 1]
        for acc, w in ((q_acc, wqb), (k_acc, wkb), (v_acc, wvb)):
            piece = dot(x, w[slot])
            acc[...] = piece if slot == 0 else acc[...] + piece

    def project_cot(slot):
        weight_copies[slot][3].wait()
        y = cot_ref[...] if slot == 0 else cs[slot - 1]
        piece = dot(y, wob[slot], NT)
        g_acc[...] = piece if slot == 0 else g_acc[...] + piece

    def group_at(g):
        return (0, 3) if isinstance(g, int) and g == 0 else (2 * g + 1, 2)

    def inner(g, act):
        lo, count = group_at(g)
        part = pl.ds(lo, count)

        def copy(dst, rcv, to):
            return remote(ad.at[part], dst.at[part], i_snd.at[g], rcv.at[g], {"tp": to})

        pl.when(col < mid - 1)(lambda: act(copy(rin, r_rcv, (col + 1) % tp)))
        pl.when(col > mid)(lambda: act(copy(rin, r_rcv, (col + tp - 1) % tp)))
        pl.when(col == mid - 1)(lambda: act(copy(xin, s_rcv, (col + 1) % tp)))
        pl.when(col == mid)(lambda: act(copy(xin, s_rcv, (col + tp - 1) % tp)))

    def outer(g, act):
        lo, count = group_at(g)
        part = pl.ds(lo, count)

        def copy(to):
            return remote(full.at[part], full.at[part], o_snd.at[g], o_rcv.at[g], {"tp": to})

        pl.when((col < mid) & (col > 0))(lambda: act(copy((col + tp - 1) % tp)))
        pl.when((col >= mid) & (col < last))(lambda: act(copy((col + 1) % tp)))

    def waits_on(buf, rcv, g):
        lo, count = group_at(g)
        part = pl.ds(lo, count)
        remote(
            buf.at[part], buf.at[part], o_snd.at[g], rcv.at[g], {"tp": (col + 1) % tp}
        ).wait_recv()

    edge = (col == 0) | (col == last)
    central = (col == mid - 1) | (col == mid)

    def publish(g):
        pl.when(edge)(lambda: inner(g, lambda c: c.start()))

    def chain(g):
        lo, count = group_at(g)
        part = pl.ds(lo, count)

        @pl.when(jnp.logical_not(edge))
        def _():
            waits_on(rin, r_rcv, g)
            ad[part] = (ad[part].astype(F32) + rin[part].astype(F32)).astype(BF16)
            inner(g, lambda c: c.start())

    def total(g):
        lo, count = group_at(g)
        part = pl.ds(lo, count)

        @pl.when(central)
        def _():
            waits_on(xin, s_rcv, g)
            full[part] = (ad[part].astype(F32) + xin[part].astype(F32)).astype(BF16)
            outer(g, lambda c: c.start())

    def totals_here(g):
        @pl.when(jnp.logical_not(central))
        def _():
            waits_on(full, o_rcv, g)
            pl.when(jnp.logical_not(edge))(lambda: outer(g, lambda c: c.start()))

    def two(own, buf, at):
        both = buf[pl.ds(at, 2)].reshape(2 * length, buf.shape[2])
        return dot(own[...], both, NT)

    def put(g, tiles):
        lo = 2 * g + 1
        ad[lo] = tiles[:, :length].astype(BF16)
        ad[lo + 1] = tiles[:, length:].astype(BF16)
        publish(g)

    def multiply_near(d):
        x_pass(d).wait_recv()
        put(2 * d - 1, two(states_ref, x_in, 2 * (d - 1)))
        c_pass(d).wait_recv()
        put(2 * d, two(cot_ref, c_in, 2 * (d - 1)))

    def multiply_far():
        far_pass().wait_recv()

        @pl.when(low_chip)
        def _():
            put(ring - 1, two(cot_ref, d_in, 0))

        @pl.when(chip >= far)
        def _():
            put(ring - 1, two(states_ref, d_in, 0))

    def multiply_own():
        ad[0] = dot(states_ref[...], states_ref[...], NT).astype(BF16)
        ad[1] = dot(cot_ref[...], cot_ref[...], NT).astype(BF16)

    def multiply_beside():
        beside_copy(states_ref).wait_recv()

        @pl.when(core == 0)
        def _():
            ad[2] = dot(states_ref[...], b_in[...], NT).astype(BF16)

        @pl.when(core == 1)
        def _():
            ad[2] = dot(cot_ref[...], b_in[...], NT).astype(BF16)

        publish(0)

    lane = lax.broadcasted_iota(jnp.int32, (length, LANES), 1)
    low = lane < HEAD_DIM
    first = lane % HEAD_DIM < HEAD_DIM // 2
    cos, sin = cos_ref[...], sin_ref[...]
    causal = lax.broadcasted_iota(jnp.int32, (length, length), 0) >= lax.broadcasted_iota(
        jnp.int32, (length, length), 1
    )

    def swap(v):
        return pltpu.roll(v, HEAD_DIM, 1)

    def rope(v):
        turned = jnp.where(
            first, pltpu.roll(v, LANES - HEAD_DIM // 2, 1), pltpu.roll(v, HEAD_DIM // 2, 1)
        )
        return v * cos + turned * sin

    def halves(v):
        other = swap(v)
        zero = jnp.zeros_like(v)
        return (
            (jnp.where(low, v, zero).astype(BF16), jnp.where(low, zero, other).astype(BF16)),
            (jnp.where(low, other, zero).astype(BF16), jnp.where(low, zero, v).astype(BF16)),
        )

    blocks = [
        (b, g, (b * 2 + g) * (GROUP // 2) + pair)
        for b in range(kv_cols // LANES)
        for g in range(2)
        for pair in range(GROUP // 2)
    ]

    def attend():
        for b, g, at in blocks:
            kcut, cut = slice(b * LANES, (b + 1) * LANES), slice(at * LANES, (at + 1) * LANES)
            keys = halves(rope(k_acc[:, kcut]))
            values = halves(v_acc[:, kcut])
            q = rope(q_acc[:, cut]).astype(BF16)
            att = None
            for side in range(2):
                s = dot(q, keys[g][side], NT) * HEAD_DIM ** (-0.5)
                s = jnp.where(causal, s, -jnp.inf)
                e = jnp.exp(s - jnp.max(s, axis=1, keepdims=True))
                p = (e / jnp.sum(e, axis=1, keepdims=True)).astype(BF16)
                probs[2 * at + side] = p
                a = dot(p, values[g][side])
                att = a if att is None else att + a
            att_own[:, cut] = att.astype(BF16)

    def grad_values():
        sums = {}
        for b, g, at in blocks:
            ga = g_acc[:, at * LANES : (at + 1) * LANES].astype(BF16)
            for side in range(2):
                u = dot(probs[2 * at + side], ga, TN)
                key = (b, g, side)
                sums[key] = sums[key] + u if key in sums else u
        for b in range(kv_cols // LANES):
            grad = jnp.where(
                low,
                sums[b, 0, 0] + swap(sums[b, 0, 1]),
                swap(sums[b, 1, 0]) + sums[b, 1, 1],
            )
            gv_own[:, b * LANES : (b + 1) * LANES] = grad.astype(BF16)

    def a_copy(d):
        return remote(
            att_own, a_in.at[2 * (d - 1)], a_snd.at[d - 1], a_rcv.at[d - 1],
            {"seq": device(d, core)},
        )

    def a_far():
        return remote(
            att_own, ad_in.at[0], a_snd.at[far - 1], a_rcv.at[far - 1],
            {"seq": device(far, core)},
        )

    def a_beside():
        return remote(att_own, ab_in, b_snd.at[1], b_rcv.at[1], {"seq": partner})

    def a_pass(d):
        return remote(
            a_in.at[2 * (d - 1)], a_in.at[2 * (d - 1) + 1], af_snd.at[d - 1],
            af_rcv.at[d - 1], {"seq": partner},
        )

    def a_far_pass():
        return remote(
            ad_in.at[0], ad_in.at[1], af_snd.at[far - 1], af_rcv.at[far - 1], {"seq": partner}
        )

    def send_attended():
        each(1, far, lambda d: a_copy(d).start())
        pl.when(chip >= far)(lambda: a_far().start())
        pl.when(core == 0)(lambda: a_beside().start())

    def pass_attended():
        def one(d):
            a_copy(d).wait_recv()
            a_pass(d).start()

        each(1, far, one)

        @pl.when(low_chip)
        def _():
            a_far().wait_recv()
            a_far_pass().start()

    def g_copy(d, other):
        return remote(
            gv_own, g_in.at[2 * (d - 1) + other], g_snd.at[other, d - 1],
            g_rcv.at[other, d - 1], {"seq": device(-d, (core + other) % 2)},
        )

    def g_far(other):
        return remote(
            gv_own, gd_in.at[other], g_snd.at[other, far - 1], g_rcv.at[other, far - 1],
            {"seq": device(far, (core + other) % 2)},
        )

    def g_beside():
        return remote(gv_own, gb_in, b_snd.at[2], b_rcv.at[2], {"seq": partner})

    def send_grads():
        @pl.when(low_chip)
        def _():
            for other in range(2):
                g_far(other).start()

        def one(d):
            for other in range(2):
                g_copy(d, other).start()

        each(1, far, one)
        pl.when(core == 1)(lambda: g_beside().start())

    lane_at = lax.broadcasted_iota(jnp.int32, (1, lanes), 1)

    def weigh(tile, b):
        product = full[tile].astype(F32) * b
        return jnp.sum(jnp.sum(product, axis=0, keepdims=True), axis=1, keepdims=True)

    def note(source, value):
        t2[col, me] += jnp.where(lane_at == source, value, 0.0)

    def score_two(g, hop, own, buf, at):
        b = two(own, buf, at)
        for other in range(2):
            note(
                device(hop, (core + other) % 2),
                weigh(2 * g + 1 + other, b[:, other * length : (other + 1) * length]),
            )

    def score_attended(d):
        a_pass(d).wait_recv()
        score_two(2 * d, -d, att_own, a_in, 2 * (d - 1))

    def score_grads(d):
        for other in range(2):
            g_copy(d, other).wait_recv()
        score_two(2 * d - 1, d, gv_own, g_in, 2 * (d - 1))

    multiply_own()
    project_states(0)
    relay(0, 1)
    follow(1)
    multiply_beside()
    settle(0, 1)
    arrivals(1, project_states)
    each(1, far, pass_near)
    if tp > 2:
        relay(0, 2)
        follow(2)
    relay(1, 1)
    each(1, far, multiply_near)
    for k in range(2, tp):
        settle(0, k)
        arrivals(k, project_states)
        if k + 1 < tp:
            relay(0, k + 1)
            follow(k + 1)
    project_cot(0)
    pass_far()
    attend()
    send_attended()
    multiply_far()
    settle(1, 1)
    arrivals(1, project_cot)
    each(0, min(ring, 2), chain)
    for k in range(2, tp):
        relay(1, k)
    each(min(ring, 2), ring, chain)
    for k in range(2, tp):
        settle(1, k)
        arrivals(k, project_cot)
        if k == 2:
            each(0, min(ring, 2), total)
    if tp <= 2:
        each(0, min(ring, 2), total)
    grad_values()
    send_grads()
    pass_attended()
    each(min(ring, 2), ring, total)
    totals_here(0)
    each(1, ring, totals_here)

    t2[col, me] = jnp.zeros((1, lanes), F32)
    note(me, weigh(1, dot(att_own[...], att_own[...], NT)))
    note(me, weigh(0, dot(gv_own[...], gv_own[...], NT)))

    @pl.when(core == 1)
    def _():
        a_beside().wait_recv()
        note(partner, weigh(2, dot(att_own[...], ab_in[...], NT)))

    @pl.when(core == 0)
    def _():
        g_beside().wait_recv()
        note(partner, weigh(2, dot(gv_own[...], gb_in[...], NT)))

    each(1, far, score_attended)

    @pl.when(low_chip)
    def _():
        a_far_pass().wait_recv()
        score_two(ring - 1, far, att_own, ad_in, 0)

    each(1, far, score_grads)

    @pl.when(chip >= far)
    def _():
        for other in range(2):
            g_far(other).wait_recv()
        score_two(ring - 1, far, gv_own, gd_in, 0)

    def r2_copy(o):
        mine = t2.at[col, me]
        to = {"seq": (me + o) % n, "tp": (col + o // n) % tp}
        return remote(mine, mine, r2_snd.at[o - 1], r2_rcv.at[o - 1], to)

    def every(act):
        if n * tp <= 32:
            for o in range(1, n * tp):
                act(r2_copy(o))
        else:
            each(1, n * tp, lambda o: act(r2_copy(o)))

    every(lambda c: c.start())
    every(lambda c: c.wait_recv())

    table = t2[0].reshape(n, lanes)
    for q in range(1, tp):
        table = table + t2[q].reshape(n, lanes)
    rank = lax.broadcasted_iota(jnp.int32, (n, lanes), 0)
    spot = lax.broadcasted_iota(jnp.int32, (n, lanes), 1)
    eye = rank == spot
    column = jnp.sum(jnp.where(spot == me, table, 0.0), axis=1, keepdims=True)
    theirs = eye & (rank != me)
    mirrored = jnp.sum(jnp.where(theirs, column, 0.0), axis=0, keepdims=True)
    own = jnp.sum(jnp.where(rank == me, table, 0.0), axis=0, keepdims=True)
    diag = jnp.sum(jnp.where(eye, table, 0.0), axis=0, keepdims=True)
    own_diag = jnp.sum(jnp.where(lane_at == me, diag, 0.0), axis=1, keepdims=True)
    gram = (own + mirrored) / jnp.sqrt(own_diag * diag)
    out_ref[...] = gram[:, :n]

    for k in range(1, tp):
        for which in range(2):
            for h in range(HALVES):
                pl.when(sends_up(k))(lambda: up(which, k, h).wait_send())
                pl.when(sends_down(k))(lambda: down(which, k, h).wait_send())

    def drain_near(d):
        for c in (x_copy(d), c_copy(d), x_pass(d), c_pass(d), a_copy(d), a_pass(d)):
            c.wait_send()
        for other in range(2):
            g_copy(d, other).wait_send()

    each(1, far, drain_near)
    far_copy(states_ref).wait_send()
    far_pass().wait_send()
    beside_copy(states_ref).wait_send()
    pl.when(chip >= far)(lambda: a_far().wait_send())
    pl.when(core == 0)(lambda: a_beside().wait_send())
    pl.when(core == 1)(lambda: g_beside().wait_send())

    @pl.when(low_chip)
    def _():
        a_far_pass().wait_send()
        for other in range(2):
            g_far(other).wait_send()

    def drain_sums(g):
        inner(g, lambda c: c.wait_send())
        outer(g, lambda c: c.wait_send())

    drain_sums(0)
    each(1, ring, drain_sums)
    every(lambda c: c.wait_send())


def on_device(n, tp, states, cotangent, wq, wk, wv, wo):
    seq_dev, length, width = states.shape
    assert seq_dev == 1 and n % 4 == 0 and length == LANES and tp > 1
    kv = wk.shape[1]
    ring = n // 2
    far = ring // 2
    near = max(far - 1, 1)
    tiles = 2 * ring + 1
    lanes = -(-n // LANES) * LANES
    cos, sin = rope_tables(length)
    vmem = pl.BlockSpec(memory_space=pltpu.VMEM)
    hbm = pl.BlockSpec(memory_space=pl.ANY)
    sem = pltpu.SemaphoreType.DMA

    def half(*shape):
        return pltpu.VMEM(shape, BF16)

    def wide(*shape):
        return pltpu.VMEM(shape, F32)

    return pl.pallas_call(
        functools.partial(kernel, n, tp),
        out_shape=jax.ShapeDtypeStruct((1, n), F32),
        in_specs=[vmem] * 4 + [hbm] * 4,
        out_specs=vmem,
        scratch_shapes=[
            half(tp - 1, length, width),
            half(tp - 1, length, width),
            half(tp, width, wq.shape[1]),
            half(tp, width, kv),
            half(tp, width, kv),
            half(tp, wo.shape[0], width),
            wide(length, wq.shape[1]),
            wide(length, kv),
            wide(length, kv),
            wide(length, wo.shape[0]),
            half(2 * near, length, width),
            half(2 * near, length, width),
            half(2, length, width),
            half(length, width),
            half(length, width),
            half(2 * near, length, width),
            half(2, length, width),
            half(length, width),
            half(length, kv),
            half(2 * near, length, kv),
            half(2, length, kv),
            half(length, kv),
            half(width // HEAD_DIM, length, length),
            half(tiles, length, length),
            half(tiles, length, length),
            half(tiles, length, length),
            half(tiles, length, length),
            wide(tp, n, 1, lanes),
            sem((4 * tp,)),
            sem((2, 2, tp - 1, HALVES)),
            sem((2, tp - 1, HALVES)),
            sem((3, far)),
            sem((3, far)),
            sem((3, far)),
            sem((3, far)),
            sem((3,)),
            sem((3,)),
            sem((far,)),
            sem((far,)),
            sem((far,)),
            sem((far,)),
            sem((2, far)),
            sem((2, far)),
            sem((ring,)),
            sem((ring,)),
            sem((ring,)),
            sem((ring,)),
            sem((ring,)),
            sem((n * tp - 1,)),
            sem((n * tp - 1,)),
        ],
        compiler_params=pltpu.CompilerParams(
            collective_id=0, has_side_effects=True, vmem_limit_bytes=60 * 1024 * 1024
        ),
        name="ntk_gram",
    )(
        states.reshape(length, width), cotangent.reshape(length, width),
        jnp.asarray(cos), jnp.asarray(sin), wq, wk, wv, wo,
    )


def solution(mesh):
    in_specs = (
        P("seq", None, "tp"),
        P("seq", None, "tp"),
        P(None, "tp"),
        P(None, "tp"),
        P(None, "tp"),
        P("tp", None),
    )
    return jax.shard_map(
        functools.partial(on_device, mesh.shape["seq"], mesh.shape["tp"]),
        mesh=mesh, in_specs=in_specs, out_specs=P("seq", None), check_vma=False,
    )
```

time: 48.1 us -> 43.1 us (0.90)
  Pallas kernels: 46.7 us -> 41.7 us
    pallas_call x1, Pallas kernels: 46.7 us -> 41.7 us  [on_device(): pl.pallas_call(functools.partial(kernel, n, tp), out_shape=jax.ShapeDtype...]
where the time goes in v1:
time: 43.1 us; the launch traced here: 42.9 us
  Pallas kernels  41.7 us (97%)
  local copies, waits for them, and re-layouts  1.19 us (3%)
    pallas_call x1, Pallas kernels, on_device(): pl.pallas_call(functools.partial(kernel, n, tp), out_shape=jax.ShapeDtype...  41.7 us
    unnamed x1, local copies, waits for them, and re-layouts  1.19 us

profile of v1, /device:TPU:0, one launch (start us, length us, event | category | flops | bytes accessed | tf_op | source)
XLA Modules:
  0.0 42.9 jit_solution(3495658575992464151)
XLA Ops:
  0.0 41.7 %ntk_gram.1 = f32[1,8]{1,0:T(1,128)} custom-call(bf16[128,512]{1,0:T(8,128)(2,1)} %bitcast.2, bf16[128,512]{1,0:T(8,128)(2,1)} %bitcast.3, f32[128,128]{1,0:T(8,128)} %constant.4.clone.cos_ref, f32[128,128]{1,0:T(8,128)} %constant.5.clone.sin_ref, bf16[2048,512]{1,0:T(8,128)(2,1)} %wq_hbm.1, bf16[2048,128]{1,0:T(8,128)(2,1)} %wk_hbm.1, ...), custom_call_target="tpu_custom_call" | custom-call | tf_op jit(solution)/shard_map/ntk_gram/pallas_call | solution.py:695
  41.7 1.2 %copy.10 = f32[1,8]{1,0:T(1,128)} copy(f32[1,8]{1,0:T(1,128)} %ntk_gram.1) | data formatting | bytes 64

commit v2 on v1

--- a/solution.py
+++ b/solution.py
@@ -57,12 +57,12 @@
 
 def kernel(
     n, tp,
-    states_ref, cot_ref, cos_ref, sin_ref, wq_hbm, wk_hbm, wv_hbm, wo_hbm,
+    states_hbm, cot_hbm, cos_hbm, sin_hbm, wq_hbm, wk_hbm, wv_hbm, wo_hbm,
     out_ref,
-    xs, cs, wqb, wkb, wvb, wob, q_acc, k_acc, v_acc, g_acc,
+    states_ref, cot_ref, cos_ref, sin_ref, xs, cs, wqb, wkb, wvb, wob, q_acc, k_acc, v_acc, g_acc,
     x_in, c_in, d_in, b_in, att_own, a_in, ad_in, ab_in, gv_own, g_in, gd_in, gb_in,
-    probs, ad, rin, xin, full, t2,
-    w_sem, z_snd, z_rcv, p_snd, p_rcv, f_snd, f_rcv, b_snd, b_rcv,
+    probs, ad, rin, xin, full, near, sums, t2,
+    in_sem, w_sem, z_snd, z_rcv, p_snd, p_rcv, f_snd, f_rcv, b_snd, b_rcv,
     a_snd, a_rcv, af_snd, af_rcv, g_snd, g_rcv,
     i_snd, r_rcv, s_rcv, o_snd, o_rcv, r2_snd, r2_rcv,
 ):
@@ -72,7 +72,7 @@
     far = ring // 2
     mid = tp // 2
     hrows = length // HALVES
-    lanes = t2.shape[3]
+    lanes = t2.shape[2]
     me = lax.axis_index("seq")
     col = lax.axis_index("tp")
     place = place_of(me, n)
@@ -97,6 +97,13 @@
             src_ref=src, dst_ref=dst, send_sem=snd, recv_sem=rcv, device_id=to
         )
 
+    input_copies = [
+        pltpu.make_async_copy(src, dst, in_sem.at[i])
+        for i, (src, dst) in enumerate((
+            (states_hbm, states_ref), (cot_hbm, cot_ref),
+            (cos_hbm, cos_ref), (sin_hbm, sin_ref),
+        ))
+    ]
     weight_copies = []
     for k in range(tp):
         at = pl.ds(pl.multiple_of(((col - k + tp) % tp) * width, width), width)
@@ -115,11 +122,15 @@
         lambda: pl.semaphore_signal(barrier, inc=1, device_id={"tp": col + 1})
     )
     each(1, n, lambda o: pl.semaphore_signal(barrier, inc=1, device_id={"seq": (me + o) % n}))
+    for c in input_copies:
+        c.start()
     order = [0] + [s for k in range(1, tp) for s in dict.fromkeys((k, tp - k)) if k <= tp - k]
     for part in (slice(0, 3), slice(3, 4)):
         for k in order:
             for c in weight_copies[k][part]:
                 c.start()
+    for c in input_copies[:2]:
+        c.wait()
     ends = (col == 0).astype(jnp.int32) + (col == last).astype(jnp.int32)
     pl.semaphore_wait(barrier, n + 1 - ends)
 
@@ -210,9 +221,6 @@
             src, d_in.at[0], p_snd.at[2, 0], p_rcv.at[2, 0], {"seq": device(far, core)}
         )
 
-    def beside_copy(src):
-        return remote(src, b_in, b_snd.at[0], b_rcv.at[0], {"seq": partner})
-
     def x_pass(d):
         return remote(
             x_in.at[2 * (d - 1)], x_in.at[2 * (d - 1) + 1], f_snd.at[0, d - 1],
@@ -234,8 +242,6 @@
         x_copy(d).start()
         c_copy(d).start()
 
-    pl.when(core == 1)(lambda: beside_copy(states_ref).start())
-    pl.when(core == 0)(lambda: beside_copy(cot_ref).start())
     each(1, far, start_near)
     pl.when(low_chip)(lambda: far_copy(states_ref).start())
     pl.when(chip >= far)(lambda: far_copy(cot_ref).start())
@@ -250,9 +256,35 @@
         far_copy(states_ref).wait_recv()
         far_pass().start()
 
+    def own_block(which, slot):
+        return inputs[which] if slot == 0 else held[which].at[slot - 1]
+
+    def beside(which, slot):
+        return remote(
+            own_block(which, slot), b_in.at[slot], b_snd.at[slot], b_rcv.at[slot],
+            {"seq": partner},
+        )
+
+    def square(which, slot):
+        x = own_block(which, slot)[...]
+        piece = dot(x, x, NT)
+        near[which] = piece if slot == 0 else near[which] + piece
+        pl.when(core == 1 - which)(lambda: beside(which, slot).start())
+
+    def multiply_beside(which):
+        @pl.when(core == which)
+        def _():
+            acc = None
+            for slot in range(tp):
+                beside(which, slot).wait_recv()
+                piece = dot(own_block(which, slot)[...], b_in[slot], NT)
+                acc = piece if acc is None else acc + piece
+            near[2] = acc
+
     def project_states(slot):
         for c in weight_copies[slot][:3]:
             c.wait()
+        square(0, slot)
         x = states_ref[...] if slot == 0 else xs[slot - 1]
         for acc, w in ((q_acc, wqb), (k_acc, wkb), (v_acc, wvb)):
             piece = dot(x, w[slot])
@@ -260,16 +292,13 @@
 
     def project_cot(slot):
         weight_copies[slot][3].wait()
+        square(1, slot)
         y = cot_ref[...] if slot == 0 else cs[slot - 1]
         piece = dot(y, wob[slot], NT)
         g_acc[...] = piece if slot == 0 else g_acc[...] + piece
 
-    def group_at(g):
-        return (0, 3) if isinstance(g, int) and g == 0 else (2 * g + 1, 2)
-
     def inner(g, act):
-        lo, count = group_at(g)
-        part = pl.ds(lo, count)
+        part = pl.ds(2 * g, 2)
 
         def copy(dst, rcv, to):
             return remote(ad.at[part], dst.at[part], i_snd.at[g], rcv.at[g], {"tp": to})
@@ -280,8 +309,7 @@
         pl.when(col == mid)(lambda: act(copy(xin, s_rcv, (col + tp - 1) % tp)))
 
     def outer(g, act):
-        lo, count = group_at(g)
-        part = pl.ds(lo, count)
+        part = pl.ds(2 * g, 2)
 
         def copy(to):
             return remote(full.at[part], full.at[part], o_snd.at[g], o_rcv.at[g], {"tp": to})
@@ -290,8 +318,7 @@
         pl.when((col >= mid) & (col < last))(lambda: act(copy((col + 1) % tp)))
 
     def waits_on(buf, rcv, g):
-        lo, count = group_at(g)
-        part = pl.ds(lo, count)
+        part = pl.ds(2 * g, 2)
         remote(
             buf.at[part], buf.at[part], o_snd.at[g], rcv.at[g], {"tp": (col + 1) % tp}
         ).wait_recv()
@@ -303,8 +330,7 @@
         pl.when(edge)(lambda: inner(g, lambda c: c.start()))
 
     def chain(g):
-        lo, count = group_at(g)
-        part = pl.ds(lo, count)
+        part = pl.ds(2 * g, 2)
 
         @pl.when(jnp.logical_not(edge))
         def _():
@@ -313,8 +339,7 @@
             inner(g, lambda c: c.start())
 
     def total(g):
-        lo, count = group_at(g)
-        part = pl.ds(lo, count)
+        part = pl.ds(2 * g, 2)
 
         @pl.when(central)
         def _():
@@ -333,48 +358,32 @@
         return dot(own[...], both, NT)
 
     def put(g, tiles):
-        lo = 2 * g + 1
-        ad[lo] = tiles[:, :length].astype(BF16)
-        ad[lo + 1] = tiles[:, length:].astype(BF16)
+        ad[2 * g] = tiles[:, :length].astype(BF16)
+        ad[2 * g + 1] = tiles[:, length:].astype(BF16)
         publish(g)
 
     def multiply_near(d):
         x_pass(d).wait_recv()
-        put(2 * d - 1, two(states_ref, x_in, 2 * (d - 1)))
+        put(2 * d - 2, two(states_ref, x_in, 2 * (d - 1)))
         c_pass(d).wait_recv()
-        put(2 * d, two(cot_ref, c_in, 2 * (d - 1)))
+        put(2 * d - 1, two(cot_ref, c_in, 2 * (d - 1)))
 
     def multiply_far():
         far_pass().wait_recv()
 
         @pl.when(low_chip)
         def _():
-            put(ring - 1, two(cot_ref, d_in, 0))
+            put(ring - 2, two(cot_ref, d_in, 0))
 
         @pl.when(chip >= far)
         def _():
-            put(ring - 1, two(states_ref, d_in, 0))
-
-    def multiply_own():
-        ad[0] = dot(states_ref[...], states_ref[...], NT).astype(BF16)
-        ad[1] = dot(cot_ref[...], cot_ref[...], NT).astype(BF16)
-
-    def multiply_beside():
-        beside_copy(states_ref).wait_recv()
-
-        @pl.when(core == 0)
-        def _():
-            ad[2] = dot(states_ref[...], b_in[...], NT).astype(BF16)
-
-        @pl.when(core == 1)
-        def _():
-            ad[2] = dot(cot_ref[...], b_in[...], NT).astype(BF16)
-
-        publish(0)
+            put(ring - 2, two(states_ref, d_in, 0))
 
     lane = lax.broadcasted_iota(jnp.int32, (length, LANES), 1)
     low = lane < HEAD_DIM
     first = lane % HEAD_DIM < HEAD_DIM // 2
+    for c in input_copies[2:]:
+        c.wait()
     cos, sin = cos_ref[...], sin_ref[...]
     causal = lax.broadcasted_iota(jnp.int32, (length, length), 0) >= lax.broadcasted_iota(
         jnp.int32, (length, length), 1
@@ -450,7 +459,7 @@
         )
 
     def a_beside():
-        return remote(att_own, ab_in, b_snd.at[1], b_rcv.at[1], {"seq": partner})
+        return remote(att_own, ab_in, b_snd.at[tp], b_rcv.at[tp], {"seq": partner})
 
     def a_pass(d):
         return remote(
@@ -493,7 +502,7 @@
         )
 
     def g_beside():
-        return remote(gv_own, gb_in, b_snd.at[2], b_rcv.at[2], {"seq": partner})
+        return remote(gv_own, gb_in, b_snd.at[tp + 1], b_rcv.at[tp + 1], {"seq": partner})
 
     def send_grads():
         @pl.when(low_chip)
@@ -510,94 +519,88 @@
 
     lane_at = lax.broadcasted_iota(jnp.int32, (1, lanes), 1)
 
-    def weigh(tile, b):
-        product = full[tile].astype(F32) * b
-        return jnp.sum(jnp.sum(product, axis=0, keepdims=True), axis=1, keepdims=True)
-
-    def note(source, value):
-        t2[col, me] += jnp.where(lane_at == source, value, 0.0)
+    def weigh(source, d, b):
+        at = pl.ds(source, 1)
+        sums[at, :] = sums[at, :] + jnp.sum(d * b, axis=0, keepdims=True)
 
     def score_two(g, hop, own, buf, at):
         b = two(own, buf, at)
         for other in range(2):
-            note(
-                device(hop, (core + other) % 2),
-                weigh(2 * g + 1 + other, b[:, other * length : (other + 1) * length]),
+            weigh(
+                device(hop, (core + other) % 2), full[2 * g + other].astype(F32),
+                b[:, other * length : (other + 1) * length],
             )
 
     def score_attended(d):
         a_pass(d).wait_recv()
-        score_two(2 * d, -d, att_own, a_in, 2 * (d - 1))
+        score_two(2 * d - 1, -d, att_own, a_in, 2 * (d - 1))
 
     def score_grads(d):
         for other in range(2):
             g_copy(d, other).wait_recv()
-        score_two(2 * d - 1, d, gv_own, g_in, 2 * (d - 1))
-
-    multiply_own()
+        score_two(2 * d - 2, d, gv_own, g_in, 2 * (d - 1))
+
+    def near_totals(g):
+        chain(g)
+        total(g)
+
     project_states(0)
     relay(0, 1)
     follow(1)
-    multiply_beside()
+    each(1, far, pass_near)
     settle(0, 1)
     arrivals(1, project_states)
-    each(1, far, pass_near)
     if tp > 2:
         relay(0, 2)
         follow(2)
+    each(1, far, multiply_near)
+    for k in range(3, tp):
+        relay(0, k)
+        follow(k)
+    pass_far()
+    project_cot(0)
     relay(1, 1)
-    each(1, far, multiply_near)
+    multiply_far()
     for k in range(2, tp):
         settle(0, k)
         arrivals(k, project_states)
-        if k + 1 < tp:
-            relay(0, k + 1)
-            follow(k + 1)
-    project_cot(0)
-    pass_far()
+    each(0, ring - 1, chain)
     attend()
     send_attended()
-    multiply_far()
     settle(1, 1)
     arrivals(1, project_cot)
-    each(0, min(ring, 2), chain)
     for k in range(2, tp):
         relay(1, k)
-    each(min(ring, 2), ring, chain)
+    each(0, ring - 1, total)
     for k in range(2, tp):
         settle(1, k)
         arrivals(k, project_cot)
-        if k == 2:
-            each(0, min(ring, 2), total)
-    if tp <= 2:
-        each(0, min(ring, 2), total)
     grad_values()
     send_grads()
+    multiply_beside(0)
+    multiply_beside(1)
     pass_attended()
-    each(min(ring, 2), ring, total)
-    totals_here(0)
-    each(1, ring, totals_here)
-
-    t2[col, me] = jnp.zeros((1, lanes), F32)
-    note(me, weigh(1, dot(att_own[...], att_own[...], NT)))
-    note(me, weigh(0, dot(gv_own[...], gv_own[...], NT)))
+    sums[...] = jnp.zeros_like(sums)
+    weigh(me, near[1], dot(att_own[...], att_own[...], NT))
+    weigh(me, near[0], dot(gv_own[...], gv_own[...], NT))
 
     @pl.when(core == 1)
     def _():
         a_beside().wait_recv()
-        note(partner, weigh(2, dot(att_own[...], ab_in[...], NT)))
+        weigh(partner, near[2], dot(att_own[...], ab_in[...], NT))
 
     @pl.when(core == 0)
     def _():
         g_beside().wait_recv()
-        note(partner, weigh(2, dot(gv_own[...], gb_in[...], NT)))
-
+        weigh(partner, near[2], dot(gv_own[...], gb_in[...], NT))
+
+    each(0, ring - 1, totals_here)
     each(1, far, score_attended)
 
     @pl.when(low_chip)
     def _():
         a_far_pass().wait_recv()
-        score_two(ring - 1, far, att_own, ad_in, 0)
+        score_two(ring - 2, far, att_own, ad_in, 0)
 
     each(1, far, score_grads)
 
@@ -605,28 +608,65 @@
     def _():
         for other in range(2):
             g_far(other).wait_recv()
-        score_two(ring - 1, far, gv_own, gd_in, 0)
+        score_two(ring - 2, far, gv_own, gd_in, 0)
+
+    row_at = lax.broadcasted_iota(jnp.int32, (n, lanes), 0)
+    spot_at = lax.broadcasted_iota(jnp.int32, (n, lanes), 1)
+    pairs = jnp.sum(sums[...], axis=1, keepdims=True)[:n]
+    t2[col * n + me] = jnp.sum(
+        jnp.where(row_at == spot_at, pairs, 0.0), axis=0, keepdims=True
+    )
 
     def r2_copy(o):
-        mine = t2.at[col, me]
+        mine = t2.at[col * n + me]
         to = {"seq": (me + o) % n, "tp": (col + o // n) % tp}
-        return remote(mine, mine, r2_snd.at[o - 1], r2_rcv.at[o - 1], to)
-
-    def every(act):
-        if n * tp <= 32:
-            for o in range(1, n * tp):
-                act(r2_copy(o))
-        else:
-            each(1, n * tp, lambda o: act(r2_copy(o)))
-
-    every(lambda c: c.start())
-    every(lambda c: c.wait_recv())
-
-    table = t2[0].reshape(n, lanes)
+        return remote(mine, mine, r2_snd.at[0], r2_rcv.at[0], to)
+
+    if n * tp <= 32:
+        for o in range(n * tp - 1, 0, -1):
+            r2_copy(o).start()
+    else:
+        each(1, n * tp, lambda o: r2_copy(o).start())
+
+    for k in range(1, tp):
+        for which in range(2):
+            for h in range(HALVES):
+                pl.when(sends_up(k))(lambda: up(which, k, h).wait_send())
+                pl.when(sends_down(k))(lambda: down(which, k, h).wait_send())
+
+    def drain_near(d):
+        for c in (x_copy(d), c_copy(d), x_pass(d), c_pass(d), a_copy(d), a_pass(d)):
+            c.wait_send()
+        for other in range(2):
+            g_copy(d, other).wait_send()
+
+    each(1, far, drain_near)
+    far_copy(states_ref).wait_send()
+    far_pass().wait_send()
+    for slot in range(tp):
+        beside(0, slot).wait_send()
+    pl.when(chip >= far)(lambda: a_far().wait_send())
+    pl.when(core == 0)(lambda: a_beside().wait_send())
+    pl.when(core == 1)(lambda: g_beside().wait_send())
+
+    @pl.when(low_chip)
+    def _():
+        a_far_pass().wait_send()
+        for other in range(2):
+            g_far(other).wait_send()
+
+    def drain_sums(g):
+        inner(g, lambda c: c.wait_send())
+        outer(g, lambda c: c.wait_send())
+
+    each(0, ring - 1, drain_sums)
+    others = t2.at[pl.ds(0, n * tp - 1)]
+    everyone = remote(others, others, r2_snd.at[0], r2_rcv.at[0], {"seq": partner})
+    everyone.wait_recv()
+    table = t2[pl.ds(0, n)].reshape(n, lanes)
     for q in range(1, tp):
-        table = table + t2[q].reshape(n, lanes)
-    rank = lax.broadcasted_iota(jnp.int32, (n, lanes), 0)
-    spot = lax.broadcasted_iota(jnp.int32, (n, lanes), 1)
+        table = table + t2[pl.ds(q * n, n)].reshape(n, lanes)
+    rank, spot = row_at, spot_at
     eye = rank == spot
     column = jnp.sum(jnp.where(spot == me, table, 0.0), axis=1, keepdims=True)
     theirs = eye & (rank != me)
@@ -636,40 +676,7 @@
     own_diag = jnp.sum(jnp.where(lane_at == me, diag, 0.0), axis=1, keepdims=True)
     gram = (own + mirrored) / jnp.sqrt(own_diag * diag)
     out_ref[...] = gram[:, :n]
-
-    for k in range(1, tp):
-        for which in range(2):
-            for h in range(HALVES):
-                pl.when(sends_up(k))(lambda: up(which, k, h).wait_send())
-                pl.when(sends_down(k))(lambda: down(which, k, h).wait_send())
-
-    def drain_near(d):
-        for c in (x_copy(d), c_copy(d), x_pass(d), c_pass(d), a_copy(d), a_pass(d)):
-            c.wait_send()
-        for other in range(2):
-            g_copy(d, other).wait_send()
-
-    each(1, far, drain_near)
-    far_copy(states_ref).wait_send()
-    far_pass().wait_send()
-    beside_copy(states_ref).wait_send()
-    pl.when(chip >= far)(lambda: a_far().wait_send())
-    pl.when(core == 0)(lambda: a_beside().wait_send())
-    pl.when(core == 1)(lambda: g_beside().wait_send())
-
-    @pl.when(low_chip)
-    def _():
-        a_far_pass().wait_send()
-        for other in range(2):
-            g_far(other).wait_send()
-
-    def drain_sums(g):
-        inner(g, lambda c: c.wait_send())
-        outer(g, lambda c: c.wait_send())
-
-    drain_sums(0)
-    each(1, ring, drain_sums)
-    every(lambda c: c.wait_send())
+    everyone.wait_send()
 
 
 def on_device(n, tp, states, cotangent, wq, wk, wv, wo):
@@ -679,7 +686,7 @@
     ring = n // 2
     far = ring // 2
     near = max(far - 1, 1)
-    tiles = 2 * ring + 1
+    tiles = 2 * (ring - 1)
     lanes = -(-n // LANES) * LANES
     cos, sin = rope_tables(length)
     vmem = pl.BlockSpec(memory_space=pltpu.VMEM)
@@ -695,9 +702,13 @@
     return pl.pallas_call(
         functools.partial(kernel, n, tp),
         out_shape=jax.ShapeDtypeStruct((1, n), F32),
-        in_specs=[vmem] * 4 + [hbm] * 4,
+        in_specs=[hbm] * 8,
         out_specs=vmem,
         scratch_shapes=[
+            half(length, width),
+            half(length, width),
+            wide(length, LANES),
+            wide(length, LANES),
             half(tp - 1, length, width),
             half(tp - 1, length, width),
             half(tp, width, wq.shape[1]),
@@ -711,7 +722,7 @@
             half(2 * near, length, width),
             half(2 * near, length, width),
             half(2, length, width),
-            half(length, width),
+            half(tp, length, width),
             half(length, width),
             half(2 * near, length, width),
             half(2, length, width),
@@ -725,7 +736,10 @@
             half(tiles, length, length),
             half(tiles, length, length),
             half(tiles, length, length),
-            wide(tp, n, 1, lanes),
+            wide(3, length, length),
+            wide(-(-n // 8) * 8, LANES),
+            wide(tp * n, 1, lanes),
+            sem((4,)),
             sem((4 * tp,)),
             sem((2, 2, tp - 1, HALVES)),
             sem((2, tp - 1, HALVES)),
@@ -733,21 +747,21 @@
             sem((3, far)),
             sem((3, far)),
             sem((3, far)),
-            sem((3,)),
-            sem((3,)),
+            sem((tp + 2,)),
+            sem((tp + 2,)),
             sem((far,)),
             sem((far,)),
             sem((far,)),
             sem((far,)),
             sem((2, far)),
             sem((2, far)),
-            sem((ring,)),
-            sem((ring,)),
-            sem((ring,)),
-            sem((ring,)),
-            sem((ring,)),
-            sem((n * tp - 1,)),
-            sem((n * tp - 1,)),
+            sem((ring - 1,)),
+            sem((ring - 1,)),
+            sem((ring - 1,)),
+            sem((ring - 1,)),
+            sem((ring - 1,)),
+            sem((1,)),
+            sem((1,)),
         ],
         compiler_params=pltpu.CompilerParams(
             collective_id=0, has_side_effects=True, vmem_limit_bytes=60 * 1024 * 1024

time: 43.1 us -> 39.5 us (0.916)
  Pallas kernels: 41.7 us -> 38.1 us
    pallas_call x1, Pallas kernels: 41.7 us -> 38.1 us  [on_device(): pl.pallas_call(functools.partial(kernel, n, tp), out_shape=jax.ShapeDtype...]
where the time goes in v2:
time: 39.5 us; the launch traced here: 39.3 us
  Pallas kernels  38.1 us (96%)
  local copies, waits for them, and re-layouts  1.19 us (3%)
    pallas_call x1, Pallas kernels, on_device(): pl.pallas_call(functools.partial(kernel, n, tp), out_shape=jax.ShapeDtype...  38.1 us
    unnamed x1, local copies, waits for them, and re-layouts  1.19 us

profile of v2, /device:TPU:0, one launch (start us, length us, event | category | flops | bytes accessed | tf_op | source)
XLA Modules:
  0.0 39.3 jit_solution(776879129706791434)
XLA Ops:
  0.0 38.1 %ntk_gram.1 = f32[1,8]{1,0:T(1,128)} custom-call(bf16[128,512]{1,0:T(8,128)(2,1)} %bitcast.2, bf16[128,512]{1,0:T(8,128)(2,1)} %bitcast.3, f32[128,128]{1,0:T(8,128)} %constant.4.clone.cos_hbm, f32[128,128]{1,0:T(8,128)} %constant.5.clone.sin_hbm, bf16[2048,512]{1,0:T(8,128)(2,1)} %wq_hbm.1, bf16[2048,128]{1,0:T(8,128)(2,1)} %wk_hbm.1, ...), custom_call_target="tpu_custom_call" | custom-call | tf_op jit(solution)/shard_map/ntk_gram/pallas_call | solution.py:702
  38.2 1.2 %copy.10 = f32[1,8]{1,0:T(1,128)} copy(f32[1,8]{1,0:T(1,128)} %ntk_gram.1) | data formatting | bytes 64

commit v3 on v2

--- a/solution.py
+++ b/solution.py
@@ -61,8 +61,8 @@
     out_ref,
     states_ref, cot_ref, cos_ref, sin_ref, xs, cs, wqb, wkb, wvb, wob, q_acc, k_acc, v_acc, g_acc,
     x_in, c_in, d_in, b_in, att_own, a_in, ad_in, ab_in, gv_own, g_in, gd_in, gb_in,
-    probs, ad, rin, xin, full, near, sums, t2,
-    in_sem, w_sem, z_snd, z_rcv, p_snd, p_rcv, f_snd, f_rcv, b_snd, b_rcv,
+    probs, ad, rin, xin, full, near, over, sums, t2,
+    in_sem, clear_sem, w_sem, z_snd, z_rcv, p_snd, p_rcv, f_snd, f_rcv, b_snd, b_rcv,
     a_snd, a_rcv, af_snd, af_rcv, g_snd, g_rcv,
     i_snd, r_rcv, s_rcv, o_snd, o_rcv, r2_snd, r2_rcv,
 ):
@@ -124,127 +124,135 @@
     each(1, n, lambda o: pl.semaphore_signal(barrier, inc=1, device_id={"seq": (me + o) % n}))
     for c in input_copies:
         c.start()
+    for c in input_copies[:2]:
+        c.wait()
+    ends = (col == 0).astype(jnp.int32) + (col == last).astype(jnp.int32)
+    pl.semaphore_wait(barrier, n + 1 - ends)
+
+    inputs = (states_ref, cot_ref)
+    held = (xs, cs)
+
+    def rows_of(h):
+        return pl.ds(h * hrows, hrows)
+
+    def up(which, k, h):
+        src = inputs[which] if k == 1 else held[which].at[k - 2]
+        return remote(
+            src.at[rows_of(h), :], held[which].at[k - 1, rows_of(h), :],
+            z_snd.at[which, 0, k - 1, h], z_rcv.at[which, k - 1, h], {"tp": (col + 1) % tp},
+        )
+
+    def down(which, k, h):
+        src = inputs[which] if k == 1 else held[which].at[tp - k]
+        return remote(
+            src.at[rows_of(h), :], held[which].at[tp - k - 1, rows_of(h), :],
+            z_snd.at[which, 1, k - 1, h], z_rcv.at[which, tp - k - 1, h],
+            {"tp": (col + tp - 1) % tp},
+        )
+
+    def sends_up(k):
+        return (col >= k - 1) & (col < last)
+
+    def sends_down(k):
+        return (col + k - 1 < tp) & (col > 0)
+
+    def landed(which, slot, h):
+        remote(
+            inputs[which].at[rows_of(h), :], held[which].at[slot - 1, rows_of(h), :],
+            z_snd.at[which, 0, 0, h], z_rcv.at[which, slot - 1, h], {"tp": (col + 1) % tp},
+        ).wait_recv()
+
+    def begin_up(which):
+        for h in range(HALVES):
+            up(which, 1, h).start()
+
+    def begin_down(which):
+        for h in range(HALVES):
+            down(which, 1, h).start()
+
+    def relay_up(which, k, side):
+        @pl.when((col >= k) & (col < last) & side)
+        def _():
+            for h in range(HALVES):
+                landed(which, k, h)
+                up(which, k + 1, h).start()
+
+    def relay_down(which, k, side):
+        @pl.when((col + k < tp) & (col > 0) & side)
+        def _():
+            for h in range(HALVES):
+                landed(which, tp - k, h)
+                down(which, k + 1, h).start()
+
+    def relay(which, k):
+        relay_up(which, k, col < mid)
+        relay_down(which, k, col >= mid)
+        relay_up(which, k, col >= mid)
+        relay_down(which, k, col < mid)
+
+    def settle(which, k):
+        for h in range(HALVES):
+            pl.when((col >= k) & (col == last))(lambda: landed(which, k, h))
+            pl.when((col + k < tp) & (col == 0))(lambda: landed(which, tp - k, h))
+
+    def arrivals(k, body):
+        pl.when(col >= k)(lambda: body(k))
+        pl.when(col + k < tp)(lambda: body(tp - k))
+
+    def follow(k):
+        pl.when((col == k) & (col < last))(lambda: begin_up(1))
+        pl.when((jnp.minimum(last - col, 1) == k) & (col > 0))(lambda: begin_down(1))
+
+    pl.when(col < last)(lambda: begin_up(0))
+    pl.when(col > 0)(lambda: begin_down(0))
+    follow(0)
+
+    def x_copy(d):
+        return remote(
+            states_ref, x_in.at[2 * (d - 1)], p_snd.at[0, d - 1], p_rcv.at[0, d - 1],
+            {"seq": device(-d, core)},
+        )
+
+    def c_copy(d):
+        return remote(
+            cot_ref, c_in.at[2 * (d - 1)], p_snd.at[1, d - 1], p_rcv.at[1, d - 1],
+            {"seq": device(d, core)},
+        )
+
+    def far_copy(src):
+        return remote(
+            src, d_in.at[0], p_snd.at[2, 0], p_rcv.at[2, 0], {"seq": device(far, core)}
+        )
+
+    def x_pass(d):
+        return remote(
+            x_in.at[2 * (d - 1)], x_in.at[2 * (d - 1) + 1], f_snd.at[0, d - 1],
+            f_rcv.at[0, d - 1], {"seq": partner},
+        )
+
+    def c_pass(d):
+        return remote(
+            c_in.at[2 * (d - 1)], c_in.at[2 * (d - 1) + 1], f_snd.at[1, d - 1],
+            f_rcv.at[1, d - 1], {"seq": partner},
+        )
+
+    def far_pass():
+        return remote(
+            d_in.at[0], d_in.at[1], f_snd.at[2, 0], f_rcv.at[2, 0], {"seq": partner}
+        )
+
+    def start_near(d):
+        x_copy(d).start()
+        c_copy(d).start()
+
+    each(1, far, start_near)
+    pl.when(low_chip)(lambda: far_copy(states_ref).start())
+    pl.when(chip >= far)(lambda: far_copy(cot_ref).start())
     order = [0] + [s for k in range(1, tp) for s in dict.fromkeys((k, tp - k)) if k <= tp - k]
     for part in (slice(0, 3), slice(3, 4)):
         for k in order:
             for c in weight_copies[k][part]:
                 c.start()
-    for c in input_copies[:2]:
-        c.wait()
-    ends = (col == 0).astype(jnp.int32) + (col == last).astype(jnp.int32)
-    pl.semaphore_wait(barrier, n + 1 - ends)
-
-    inputs = (states_ref, cot_ref)
-    held = (xs, cs)
-
-    def rows_of(h):
-        return pl.ds(h * hrows, hrows)
-
-    def up(which, k, h):
-        src = inputs[which] if k == 1 else held[which].at[k - 2]
-        return remote(
-            src.at[rows_of(h), :], held[which].at[k - 1, rows_of(h), :],
-            z_snd.at[which, 0, k - 1, h], z_rcv.at[which, k - 1, h], {"tp": (col + 1) % tp},
-        )
-
-    def down(which, k, h):
-        src = inputs[which] if k == 1 else held[which].at[tp - k]
-        return remote(
-            src.at[rows_of(h), :], held[which].at[tp - k - 1, rows_of(h), :],
-            z_snd.at[which, 1, k - 1, h], z_rcv.at[which, tp - k - 1, h],
-            {"tp": (col + tp - 1) % tp},
-        )
-
-    def sends_up(k):
-        return (col >= k - 1) & (col < last)
-
-    def sends_down(k):
-        return (col + k - 1 < tp) & (col > 0)
-
-    def landed(which, slot, h):
-        remote(
-            inputs[which].at[rows_of(h), :], held[which].at[slot - 1, rows_of(h), :],
-            z_snd.at[which, 0, 0, h], z_rcv.at[which, slot - 1, h], {"tp": (col + 1) % tp},
-        ).wait_recv()
-
-    def begin_up(which):
-        for h in range(HALVES):
-            up(which, 1, h).start()
-
-    def begin_down(which):
-        for h in range(HALVES):
-            down(which, 1, h).start()
-
-    def relay(which, k):
-        for h in range(HALVES):
-            @pl.when((col >= k) & (col < last))
-            def _():
-                landed(which, k, h)
-                up(which, k + 1, h).start()
-
-            @pl.when((col + k < tp) & (col > 0))
-            def _():
-                landed(which, tp - k, h)
-                down(which, k + 1, h).start()
-
-    def settle(which, k):
-        for h in range(HALVES):
-            pl.when((col >= k) & (col == last))(lambda: landed(which, k, h))
-            pl.when((col + k < tp) & (col == 0))(lambda: landed(which, tp - k, h))
-
-    def arrivals(k, body):
-        pl.when(col >= k)(lambda: body(k))
-        pl.when(col + k < tp)(lambda: body(tp - k))
-
-    def follow(k):
-        pl.when((col == k) & (col < last))(lambda: begin_up(1))
-        pl.when((last - col == k) & (col > 0))(lambda: begin_down(1))
-
-    pl.when(col < last)(lambda: begin_up(0))
-    pl.when(col > 0)(lambda: begin_down(0))
-    follow(0)
-
-    def x_copy(d):
-        return remote(
-            states_ref, x_in.at[2 * (d - 1)], p_snd.at[0, d - 1], p_rcv.at[0, d - 1],
-            {"seq": device(-d, core)},
-        )
-
-    def c_copy(d):
-        return remote(
-            cot_ref, c_in.at[2 * (d - 1)], p_snd.at[1, d - 1], p_rcv.at[1, d - 1],
-            {"seq": device(d, core)},
-        )
-
-    def far_copy(src):
-        return remote(
-            src, d_in.at[0], p_snd.at[2, 0], p_rcv.at[2, 0], {"seq": device(far, core)}
-        )
-
-    def x_pass(d):
-        return remote(
-            x_in.at[2 * (d - 1)], x_in.at[2 * (d - 1) + 1], f_snd.at[0, d - 1],
-            f_rcv.at[0, d - 1], {"seq": partner},
-        )
-
-    def c_pass(d):
-        return remote(
-            c_in.at[2 * (d - 1)], c_in.at[2 * (d - 1) + 1], f_snd.at[1, d - 1],
-            f_rcv.at[1, d - 1], {"seq": partner},
-        )
-
-    def far_pass():
-        return remote(
-            d_in.at[0], d_in.at[1], f_snd.at[2, 0], f_rcv.at[2, 0], {"seq": partner}
-        )
-
-    def start_near(d):
-        x_copy(d).start()
-        c_copy(d).start()
-
-    each(1, far, start_near)
-    pl.when(low_chip)(lambda: far_copy(states_ref).start())
-    pl.when(chip >= far)(lambda: far_copy(cot_ref).start())
 
     def pass_near(d):
         x_copy(d).wait_recv()
@@ -265,10 +273,15 @@
             {"seq": partner},
         )
 
-    def square(which, slot):
-        x = own_block(which, slot)[...]
-        piece = dot(x, x, NT)
-        near[which] = piece if slot == 0 else near[which] + piece
+    def square(which, slots):
+        acc = None
+        for slot in slots:
+            x = own_block(which, slot)[...]
+            piece = dot(x, x, NT)
+            acc = piece if acc is None else acc + piece
+        near[which] = acc
+
+    def hand_over(which, slot):
         pl.when(core == 1 - which)(lambda: beside(which, slot).start())
 
     def multiply_beside(which):
@@ -284,7 +297,7 @@
     def project_states(slot):
         for c in weight_copies[slot][:3]:
             c.wait()
-        square(0, slot)
+        hand_over(0, slot)
         x = states_ref[...] if slot == 0 else xs[slot - 1]
         for acc, w in ((q_acc, wqb), (k_acc, wkb), (v_acc, wvb)):
             piece = dot(x, w[slot])
@@ -292,7 +305,7 @@
 
     def project_cot(slot):
         weight_copies[slot][3].wait()
-        square(1, slot)
+        hand_over(1, slot)
         y = cot_ref[...] if slot == 0 else cs[slot - 1]
         piece = dot(y, wob[slot], NT)
         g_acc[...] = piece if slot == 0 else g_acc[...] + piece
@@ -345,7 +358,33 @@
         def _():
             waits_on(xin, s_rcv, g)
             full[part] = (ad[part].astype(F32) + xin[part].astype(F32)).astype(BF16)
-            outer(g, lambda c: c.start())
+
+    def last_relays():
+        for h in range(HALVES):
+            @pl.when((col >= mid) & (col < last))
+            def _():
+                remote(
+                    held[1].at[col - 1, rows_of(h), :], held[1].at[col, rows_of(h), :],
+                    z_snd.at[1, 0, col, h], z_rcv.at[1, col, h], {"tp": (col + 1) % tp},
+                ).wait_send()
+
+            @pl.when((col < mid) & (col > 0))
+            def _():
+                remote(
+                    held[1].at[col, rows_of(h), :], held[1].at[col - 1, rows_of(h), :],
+                    z_snd.at[1, 1, last - col, h], z_rcv.at[1, col - 1, h],
+                    {"tp": (col + tp - 1) % tp},
+                ).wait_send()
+
+    def send_totals():
+        inside = jnp.logical_not(edge)
+        pl.when(inside & (core == 1))(lambda: pl.semaphore_wait(clear_sem, 1))
+        pl.when(central)(lambda: each(0, ring - 1, lambda g: outer(g, lambda c: c.start())))
+
+        @pl.when(inside & (core == 0))
+        def _():
+            last_relays()
+            pl.semaphore_signal(clear_sem, inc=1, device_id={"seq": partner})
 
     def totals_here(g):
         @pl.when(jnp.logical_not(central))
@@ -523,27 +562,42 @@
         at = pl.ds(source, 1)
         sums[at, :] = sums[at, :] + jnp.sum(d * b, axis=0, keepdims=True)
 
-    def score_two(g, hop, own, buf, at):
-        b = two(own, buf, at)
+    def overlap_attended(d):
+        a_pass(d).wait_recv()
+        over[2 * d - 1] = two(att_own, a_in, 2 * (d - 1))
+
+    def overlap_grads(d):
+        for other in range(2):
+            g_copy(d, other).wait_recv()
+        over[2 * d - 2] = two(gv_own, g_in, 2 * (d - 1))
+
+    def overlap_far_attended():
+        @pl.when(low_chip)
+        def _():
+            a_far_pass().wait_recv()
+            over[ring - 2] = two(att_own, ad_in, 0)
+
+    def overlap_far_grads():
+        @pl.when(chip >= far)
+        def _():
+            for other in range(2):
+                g_far(other).wait_recv()
+            over[ring - 2] = two(gv_own, gd_in, 0)
+
+    def score(g, hop):
         for other in range(2):
             weigh(
                 device(hop, (core + other) % 2), full[2 * g + other].astype(F32),
-                b[:, other * length : (other + 1) * length],
+                over[g, :, other * length : (other + 1) * length],
             )
 
-    def score_attended(d):
-        a_pass(d).wait_recv()
-        score_two(2 * d - 1, -d, att_own, a_in, 2 * (d - 1))
-
-    def score_grads(d):
-        for other in range(2):
-            g_copy(d, other).wait_recv()
-        score_two(2 * d - 2, d, gv_own, g_in, 2 * (d - 1))
-
-    def near_totals(g):
-        chain(g)
-        total(g)
-
+    def score_near(d):
+        totals_here(2 * d - 2)
+        score(2 * d - 2, d)
+        totals_here(2 * d - 1)
+        score(2 * d - 1, -d)
+
+    lower, upper, anywhere = col < mid, col >= mid, col >= 0
     project_states(0)
     relay(0, 1)
     follow(1)
@@ -551,64 +605,67 @@
     settle(0, 1)
     arrivals(1, project_states)
     if tp > 2:
-        relay(0, 2)
+        relay_up(0, 2, anywhere)
         follow(2)
     each(1, far, multiply_near)
+    relay_up(1, 1, lower)
+    relay_down(1, 1, upper)
+    if tp > 2:
+        relay_down(0, 2, anywhere)
     for k in range(3, tp):
         relay(0, k)
         follow(k)
+    project_cot(0)
+    relay_up(1, 1, upper)
     pass_far()
-    project_cot(0)
-    relay(1, 1)
-    multiply_far()
-    for k in range(2, tp):
+    for k in range(2, tp - 1):
         settle(0, k)
         arrivals(k, project_states)
-    each(0, ring - 1, chain)
+    multiply_far()
+    each(0, ring - 2, chain)
+    relay_down(1, 1, lower)
+    for k in range(2, tp):
+        relay(1, k)
+    chain(ring - 2)
+    for k in range(max(2, tp - 1), tp):
+        settle(0, k)
+        arrivals(k, project_states)
     attend()
     send_attended()
-    settle(1, 1)
-    arrivals(1, project_cot)
-    for k in range(2, tp):
-        relay(1, k)
-    each(0, ring - 1, total)
-    for k in range(2, tp):
+    square(0, range(tp))
+    for k in range(1, tp):
         settle(1, k)
         arrivals(k, project_cot)
     grad_values()
     send_grads()
+    each(0, ring - 1, total)
+    send_totals()
+    square(1, range(tp))
     multiply_beside(0)
-    multiply_beside(1)
     pass_attended()
     sums[...] = jnp.zeros_like(sums)
     weigh(me, near[1], dot(att_own[...], att_own[...], NT))
     weigh(me, near[0], dot(gv_own[...], gv_own[...], NT))
 
+    @pl.when(core == 0)
+    def _():
+        g_beside().wait_recv()
+        weigh(partner, near[2], dot(gv_own[...], gb_in[...], NT))
+
+    each(1, far, overlap_attended)
+    overlap_far_attended()
+    multiply_beside(1)
+
     @pl.when(core == 1)
     def _():
         a_beside().wait_recv()
         weigh(partner, near[2], dot(att_own[...], ab_in[...], NT))
 
-    @pl.when(core == 0)
-    def _():
-        g_beside().wait_recv()
-        weigh(partner, near[2], dot(gv_own[...], gb_in[...], NT))
-
-    each(0, ring - 1, totals_here)
-    each(1, far, score_attended)
-
-    @pl.when(low_chip)
-    def _():
-        a_far_pass().wait_recv()
-        score_two(ring - 2, far, att_own, ad_in, 0)
-
-    each(1, far, score_grads)
-
-    @pl.when(chip >= far)
-    def _():
-        for other in range(2):
-            g_far(other).wait_recv()
-        score_two(ring - 2, far, gv_own, gd_in, 0)
+    each(1, far, overlap_grads)
+    overlap_far_grads()
+    each(1, far, score_near)
+    totals_here(ring - 2)
+    score(ring - 2, far)
 
     row_at = lax.broadcasted_iota(jnp.int32, (n, lanes), 0)
     spot_at = lax.broadcasted_iota(jnp.int32, (n, lanes), 1)
@@ -617,22 +674,23 @@
         jnp.where(row_at == spot_at, pairs, 0.0), axis=0, keepdims=True
     )
 
-    def r2_copy(o):
+    def send_scalars(plane, o):
         mine = t2.at[col * n + me]
-        to = {"seq": (me + o) % n, "tp": (col + o // n) % tp}
-        return remote(mine, mine, r2_snd.at[0], r2_rcv.at[0], to)
-
-    if n * tp <= 32:
-        for o in range(n * tp - 1, 0, -1):
-            r2_copy(o).start()
-    else:
-        each(1, n * tp, lambda o: r2_copy(o).start())
+        to = {"seq": (me + o) % n, "tp": plane}
+        remote(mine, mine, r2_snd.at[0], r2_rcv.at[0], to).start()
+
+    for t in range(tp):
+        plane = jnp.where(col >= mid, t, last - t)
+        each(1, n, lambda o: send_scalars(plane, o))
+        pl.when(plane != col)(lambda: send_scalars(plane, 0))
 
     for k in range(1, tp):
         for which in range(2):
             for h in range(HALVES):
-                pl.when(sends_up(k))(lambda: up(which, k, h).wait_send())
-                pl.when(sends_down(k))(lambda: down(which, k, h).wait_send())
+                done_up = which * (k == col + 1) * (col >= mid) * (core == 0)
+                done_down = which * (k == tp - col) * (col < mid) * (core == 0)
+                pl.when(sends_up(k) & (done_up == 0))(lambda: up(which, k, h).wait_send())
+                pl.when(sends_down(k) & (done_down == 0))(lambda: down(which, k, h).wait_send())
 
     def drain_near(d):
         for c in (x_copy(d), c_copy(d), x_pass(d), c_pass(d), a_copy(d), a_pass(d)):
@@ -737,9 +795,11 @@
             half(tiles, length, length),
             half(tiles, length, length),
             wide(3, length, length),
+            wide(ring - 1, length, 2 * length),
             wide(-(-n // 8) * 8, LANES),
             wide(tp * n, 1, lanes),
             sem((4,)),
+            pltpu.SemaphoreType.REGULAR,
             sem((4 * tp,)),
             sem((2, 2, tp - 1, HALVES)),
             sem((2, tp - 1, HALVES)),

time: 39.5 us -> 37.8 us (0.957)
  Pallas kernels: 38.1 us -> 36.4 us
    pallas_call x1, Pallas kernels: 38.1 us -> 36.4 us  [on_device(): pl.pallas_call(functools.partial(kernel, n, tp), out_shape=jax.ShapeDtype...]
where the time goes in v3:
time: 37.8 us; the launch traced here: 37.6 us
  Pallas kernels  36.4 us (96%)
  local copies, waits for them, and re-layouts  1.19 us (3%)
    pallas_call x1, Pallas kernels, on_device(): pl.pallas_call(functools.partial(kernel, n, tp), out_shape=jax.ShapeDtype...  36.4 us
    unnamed x1, local copies, waits for them, and re-layouts  1.19 us

profile of v3, /device:TPU:0, one launch (start us, length us, event | category | flops | bytes accessed | tf_op | source)
XLA Modules:
  0.0 37.6 jit_solution(17199634829531930822)
XLA Ops:
  0.0 36.4 %ntk_gram.1 = f32[1,8]{1,0:T(1,128)} custom-call(bf16[128,512]{1,0:T(8,128)(2,1)} %bitcast.2, bf16[128,512]{1,0:T(8,128)(2,1)} %bitcast.3, f32[128,128]{1,0:T(8,128)} %constant.4.clone.cos_hbm, f32[128,128]{1,0:T(8,128)} %constant.5.clone.sin_hbm, bf16[2048,512]{1,0:T(8,128)(2,1)} %wq_hbm.1, bf16[2048,128]{1,0:T(8,128)(2,1)} %wk_hbm.1, ...), custom_call_target="tpu_custom_call" | custom-call | tf_op jit(solution)/shard_map/ntk_gram/pallas_call | solution.py:760
  36.5 1.2 %copy.10 = f32[1,8]{1,0:T(1,128)} copy(f32[1,8]{1,0:T(1,128)} %ntk_gram.1) | data formatting | bytes 64

commit v4 on v3

--- a/solution.py
+++ b/solution.py
@@ -184,6 +184,15 @@
                 landed(which, tp - k, h)
                 down(which, k + 1, h).start()
 
+    def relay_first():
+        for h in range(HALVES):
+            @pl.when((col > 0) & (col < last))
+            def _():
+                landed(0, 1, h)
+                up(0, 2, h).start()
+                landed(0, tp - 1, h)
+                down(0, 2, h).start()
+
     def relay(which, k):
         relay_up(which, k, col < mid)
         relay_down(which, k, col >= mid)
@@ -599,7 +608,7 @@
 
     lower, upper, anywhere = col < mid, col >= mid, col >= 0
     project_states(0)
-    relay(0, 1)
+    relay_first()
     follow(1)
     each(1, far, pass_near)
     settle(0, 1)
@@ -759,7 +768,7 @@
 
     return pl.pallas_call(
         functools.partial(kernel, n, tp),
-        out_shape=jax.ShapeDtypeStruct((1, n), F32),
+        out_shape=pltpu.VMEM((1, n), F32),
         in_specs=[hbm] * 8,
         out_specs=vmem,
         scratch_shapes=[

time: 37.8 us -> 35.3 us (0.934)
  Pallas kernels: 36.4 us -> 34.6 us
  local copies, waits for them, and re-layouts: 1.19 us -> 0.51 us
    pallas_call x1, Pallas kernels: 36.4 us -> 34.6 us  [on_device(): pl.pallas_call(functools.partial(kernel, n, tp), out_shape=pltpu.VMEM((1,...]
    unnamed x1, local copies, waits for them, and re-layouts: 1.19 us -> 0.51 us
where the time goes in v4:
time: 35.3 us; the launch traced here: 35.1 us
  Pallas kernels  34.6 us (98%)
  local copies, waits for them, and re-layouts  0.51 us (1%)
    pallas_call x1, Pallas kernels, on_device(): pl.pallas_call(functools.partial(kernel, n, tp), out_shape=pltpu.VMEM((1,...  34.6 us

profile of v4, /device:TPU:0, one launch (start us, length us, event | category | flops | bytes accessed | tf_op | source)
XLA Modules:
  0.0 35.1 jit_solution(12491679620309907662)
XLA Ops:
  0.0 34.6 %ntk_gram.1 = f32[1,8]{1,0:T(1,128)S(1)} custom-call(bf16[128,512]{1,0:T(8,128)(2,1)} %bitcast.2, bf16[128,512]{1,0:T(8,128)(2,1)} %bitcast.3, f32[128,128]{1,0:T(8,128)} %constant.4.clone.cos_hbm, f32[128,128]{1,0:T(8,128)} %constant.5.clone.sin_hbm, bf16[2048,512]{1,0:T(8,128)(2,1)} %wq_hbm.1, bf16[2048,128]{1,0:T(8,128)(2,1)} %wk_hbm.1, ...), custom_call_target="tpu_custom_call" | custom-call | tf_op jit(solution)/shard_map/ntk_gram/pallas_call | solution.py:769
  34.6 0.5 %copy.10 = f32[1,8]{1,0:T(1,128)} copy(f32[1,8]{1,0:T(1,128)S(1)} %ntk_gram.1) | data formatting | bytes 64

commit v5 on v4

--- a/solution.py
+++ b/solution.py
@@ -59,15 +59,16 @@
     n, tp,
     states_hbm, cot_hbm, cos_hbm, sin_hbm, wq_hbm, wk_hbm, wv_hbm, wo_hbm,
     out_ref,
-    states_ref, cot_ref, cos_ref, sin_ref, xs, cs, wqb, wkb, wvb, wob, q_acc, k_acc, v_acc, g_acc,
+    own, tables, xs, cs, wqkv, wob, qkv_acc, g_acc,
     x_in, c_in, d_in, b_in, att_own, a_in, ad_in, ab_in, gv_own, g_in, gd_in, gb_in,
     probs, ad, rin, xin, full, near, over, sums, t2,
-    in_sem, clear_sem, w_sem, z_snd, z_rcv, p_snd, p_rcv, f_snd, f_rcv, b_snd, b_rcv,
-    a_snd, a_rcv, af_snd, af_rcv, g_snd, g_rcv,
-    i_snd, r_rcv, s_rcv, o_snd, o_rcv, r2_snd, r2_rcv,
+    in_sem, clear_sem, w_sem, snd, last_snd, z_rcv, p_rcv, pd_rcv, f_rcv, fd_rcv, b_rcv,
+    a_rcv, af_rcv, g_rcv, r_rcv, s_rcv, o_rcv, r2_snd, r2_rcv,
 ):
+    states_ref, cot_ref = own.at[0], own.at[1]
     length, width = states_ref.shape
-    kv_cols = k_acc.shape[1]
+    q_cols = wq_hbm.shape[1]
+    kv_cols = wk_hbm.shape[1]
     ring = n // 2
     far = ring // 2
     mid = tp // 2
@@ -97,22 +98,20 @@
             src_ref=src, dst_ref=dst, send_sem=snd, recv_sem=rcv, device_id=to
         )
 
+    local = pltpu.make_async_copy
     input_copies = [
-        pltpu.make_async_copy(src, dst, in_sem.at[i])
-        for i, (src, dst) in enumerate((
-            (states_hbm, states_ref), (cot_hbm, cot_ref),
-            (cos_hbm, cos_ref), (sin_hbm, sin_ref),
-        ))
+        local(states_hbm, own.at[0], in_sem.at[0]),
+        local(cot_hbm, own.at[1], in_sem.at[0]),
+        local(cos_hbm, tables.at[0], in_sem.at[1]),
+        local(sin_hbm, tables.at[1], in_sem.at[1]),
     ]
-    weight_copies = []
-    for k in range(tp):
-        at = pl.ds(pl.multiple_of(((col - k + tp) % tp) * width, width), width)
-        weight_copies.append([
-            pltpu.make_async_copy(wq_hbm.at[at, :], wqb.at[k], w_sem.at[4 * k]),
-            pltpu.make_async_copy(wk_hbm.at[at, :], wkb.at[k], w_sem.at[4 * k + 1]),
-            pltpu.make_async_copy(wv_hbm.at[at, :], wvb.at[k], w_sem.at[4 * k + 2]),
-            pltpu.make_async_copy(wo_hbm.at[:, at], wob.at[k], w_sem.at[4 * k + 3]),
-        ])
+    kv_at = q_cols + kv_cols
+    weight_copies = [
+        local(wq_hbm, wqkv.at[:, pl.ds(0, q_cols)], w_sem.at[0]),
+        local(wk_hbm, wqkv.at[:, pl.ds(q_cols, kv_cols)], w_sem.at[0]),
+        local(wv_hbm, wqkv.at[:, pl.ds(kv_at, kv_cols)], w_sem.at[0]),
+        local(wo_hbm, wob, w_sem.at[1]),
+    ]
 
     barrier = pltpu.get_barrier_semaphore()
     pl.when(col > 0)(
@@ -124,8 +123,7 @@
     each(1, n, lambda o: pl.semaphore_signal(barrier, inc=1, device_id={"seq": (me + o) % n}))
     for c in input_copies:
         c.start()
-    for c in input_copies[:2]:
-        c.wait()
+    local(own, own, in_sem.at[0]).wait()
     ends = (col == 0).astype(jnp.int32) + (col == last).astype(jnp.int32)
     pl.semaphore_wait(barrier, n + 1 - ends)
 
@@ -135,18 +133,18 @@
     def rows_of(h):
         return pl.ds(h * hrows, hrows)
 
-    def up(which, k, h):
+    def up(which, k, h, sem=None):
         src = inputs[which] if k == 1 else held[which].at[k - 2]
         return remote(
             src.at[rows_of(h), :], held[which].at[k - 1, rows_of(h), :],
-            z_snd.at[which, 0, k - 1, h], z_rcv.at[which, k - 1, h], {"tp": (col + 1) % tp},
-        )
-
-    def down(which, k, h):
+            snd.at[0] if sem is None else sem, z_rcv.at[which, k - 1, h], {"tp": (col + 1) % tp},
+        )
+
+    def down(which, k, h, sem=None):
         src = inputs[which] if k == 1 else held[which].at[tp - k]
         return remote(
             src.at[rows_of(h), :], held[which].at[tp - k - 1, rows_of(h), :],
-            z_snd.at[which, 1, k - 1, h], z_rcv.at[which, tp - k - 1, h],
+            snd.at[0] if sem is None else sem, z_rcv.at[which, tp - k - 1, h],
             {"tp": (col + tp - 1) % tp},
         )
 
@@ -159,7 +157,7 @@
     def landed(which, slot, h):
         remote(
             inputs[which].at[rows_of(h), :], held[which].at[slot - 1, rows_of(h), :],
-            z_snd.at[which, 0, 0, h], z_rcv.at[which, slot - 1, h], {"tp": (col + 1) % tp},
+            snd.at[0], z_rcv.at[which, slot - 1, h], {"tp": (col + 1) % tp},
         ).wait_recv()
 
     def begin_up(which):
@@ -170,19 +168,29 @@
         for h in range(HALVES):
             down(which, 1, h).start()
 
+    def ends_up(which, k):
+        return (which == 1) & (k == col) & (col >= mid)
+
+    def ends_down(which, k):
+        return (which == 1) & (k == last - col) & (col < mid)
+
     def relay_up(which, k, side):
         @pl.when((col >= k) & (col < last) & side)
         def _():
             for h in range(HALVES):
                 landed(which, k, h)
-                up(which, k + 1, h).start()
+                ends = ends_up(which, k)
+                pl.when(ends)(lambda: up(which, k + 1, h, last_snd.at[h]).start())
+                pl.when(jnp.logical_not(ends))(lambda: up(which, k + 1, h).start())
 
     def relay_down(which, k, side):
         @pl.when((col + k < tp) & (col > 0) & side)
         def _():
             for h in range(HALVES):
                 landed(which, tp - k, h)
-                down(which, k + 1, h).start()
+                ends = ends_down(which, k)
+                pl.when(ends)(lambda: down(which, k + 1, h, last_snd.at[h]).start())
+                pl.when(jnp.logical_not(ends))(lambda: down(which, k + 1, h).start())
 
     def relay_first():
         for h in range(HALVES):
@@ -218,36 +226,36 @@
 
     def x_copy(d):
         return remote(
-            states_ref, x_in.at[2 * (d - 1)], p_snd.at[0, d - 1], p_rcv.at[0, d - 1],
+            states_ref, x_in.at[2 * (d - 1)], snd.at[0], p_rcv.at[0, d - 1],
             {"seq": device(-d, core)},
         )
 
     def c_copy(d):
         return remote(
-            cot_ref, c_in.at[2 * (d - 1)], p_snd.at[1, d - 1], p_rcv.at[1, d - 1],
+            cot_ref, c_in.at[2 * (d - 1)], snd.at[0], p_rcv.at[1, d - 1],
             {"seq": device(d, core)},
         )
 
     def far_copy(src):
         return remote(
-            src, d_in.at[0], p_snd.at[2, 0], p_rcv.at[2, 0], {"seq": device(far, core)}
+            src, d_in.at[0], snd.at[0], pd_rcv.at[0], {"seq": device(far, core)}
         )
 
     def x_pass(d):
         return remote(
-            x_in.at[2 * (d - 1)], x_in.at[2 * (d - 1) + 1], f_snd.at[0, d - 1],
+            x_in.at[2 * (d - 1)], x_in.at[2 * (d - 1) + 1], snd.at[0],
             f_rcv.at[0, d - 1], {"seq": partner},
         )
 
     def c_pass(d):
         return remote(
-            c_in.at[2 * (d - 1)], c_in.at[2 * (d - 1) + 1], f_snd.at[1, d - 1],
+            c_in.at[2 * (d - 1)], c_in.at[2 * (d - 1) + 1], snd.at[0],
             f_rcv.at[1, d - 1], {"seq": partner},
         )
 
     def far_pass():
         return remote(
-            d_in.at[0], d_in.at[1], f_snd.at[2, 0], f_rcv.at[2, 0], {"seq": partner}
+            d_in.at[0], d_in.at[1], snd.at[0], fd_rcv.at[0], {"seq": partner}
         )
 
     def start_near(d):
@@ -257,11 +265,8 @@
     each(1, far, start_near)
     pl.when(low_chip)(lambda: far_copy(states_ref).start())
     pl.when(chip >= far)(lambda: far_copy(cot_ref).start())
-    order = [0] + [s for k in range(1, tp) for s in dict.fromkeys((k, tp - k)) if k <= tp - k]
-    for part in (slice(0, 3), slice(3, 4)):
-        for k in order:
-            for c in weight_copies[k][part]:
-                c.start()
+    for c in weight_copies:
+        c.start()
 
     def pass_near(d):
         x_copy(d).wait_recv()
@@ -278,7 +283,7 @@
 
     def beside(which, slot):
         return remote(
-            own_block(which, slot), b_in.at[slot], b_snd.at[slot], b_rcv.at[slot],
+            own_block(which, slot), b_in.at[slot], snd.at[0], b_rcv.at[0],
             {"seq": partner},
         )
 
@@ -297,33 +302,34 @@
         @pl.when(core == which)
         def _():
             acc = None
+            remote(b_in, b_in, snd.at[0], b_rcv.at[0], {"seq": partner}).wait_recv()
             for slot in range(tp):
-                beside(which, slot).wait_recv()
                 piece = dot(own_block(which, slot)[...], b_in[slot], NT)
                 acc = piece if acc is None else acc + piece
             near[2] = acc
 
+    def features(slot):
+        return pl.ds(pl.multiple_of(((col - slot + tp) % tp) * width, width), width)
+
     def project_states(slot):
-        for c in weight_copies[slot][:3]:
-            c.wait()
+        if slot == 0:
+            local(wqkv, wqkv, w_sem.at[0]).wait()
         hand_over(0, slot)
-        x = states_ref[...] if slot == 0 else xs[slot - 1]
-        for acc, w in ((q_acc, wqb), (k_acc, wkb), (v_acc, wvb)):
-            piece = dot(x, w[slot])
-            acc[...] = piece if slot == 0 else acc[...] + piece
+        piece = dot(own_block(0, slot)[...], wqkv[features(slot), :])
+        qkv_acc[...] = piece if slot == 0 else qkv_acc[...] + piece
 
     def project_cot(slot):
-        weight_copies[slot][3].wait()
+        if slot == 0:
+            local(wob, wob, w_sem.at[1]).wait()
         hand_over(1, slot)
-        y = cot_ref[...] if slot == 0 else cs[slot - 1]
-        piece = dot(y, wob[slot], NT)
+        piece = dot(own_block(1, slot)[...], wob[:, features(slot)], NT)
         g_acc[...] = piece if slot == 0 else g_acc[...] + piece
 
     def inner(g, act):
         part = pl.ds(2 * g, 2)
 
         def copy(dst, rcv, to):
-            return remote(ad.at[part], dst.at[part], i_snd.at[g], rcv.at[g], {"tp": to})
+            return remote(ad.at[part], dst.at[part], snd.at[0], rcv.at[g], {"tp": to})
 
         pl.when(col < mid - 1)(lambda: act(copy(rin, r_rcv, (col + 1) % tp)))
         pl.when(col > mid)(lambda: act(copy(rin, r_rcv, (col + tp - 1) % tp)))
@@ -334,7 +340,7 @@
         part = pl.ds(2 * g, 2)
 
         def copy(to):
-            return remote(full.at[part], full.at[part], o_snd.at[g], o_rcv.at[g], {"tp": to})
+            return remote(full.at[part], full.at[part], snd.at[0], o_rcv.at[g], {"tp": to})
 
         pl.when((col < mid) & (col > 0))(lambda: act(copy((col + tp - 1) % tp)))
         pl.when((col >= mid) & (col < last))(lambda: act(copy((col + 1) % tp)))
@@ -342,7 +348,7 @@
     def waits_on(buf, rcv, g):
         part = pl.ds(2 * g, 2)
         remote(
-            buf.at[part], buf.at[part], o_snd.at[g], rcv.at[g], {"tp": (col + 1) % tp}
+            buf.at[part], buf.at[part], snd.at[0], rcv.at[g], {"tp": (col + 1) % tp}
         ).wait_recv()
 
     edge = (col == 0) | (col == last)
@@ -374,14 +380,14 @@
             def _():
                 remote(
                     held[1].at[col - 1, rows_of(h), :], held[1].at[col, rows_of(h), :],
-                    z_snd.at[1, 0, col, h], z_rcv.at[1, col, h], {"tp": (col + 1) % tp},
+                    last_snd.at[h], z_rcv.at[1, col, h], {"tp": (col + 1) % tp},
                 ).wait_send()
 
             @pl.when((col < mid) & (col > 0))
             def _():
                 remote(
                     held[1].at[col, rows_of(h), :], held[1].at[col - 1, rows_of(h), :],
-                    z_snd.at[1, 1, last - col, h], z_rcv.at[1, col - 1, h],
+                    last_snd.at[h], z_rcv.at[1, col - 1, h],
                     {"tp": (col + tp - 1) % tp},
                 ).wait_send()
 
@@ -430,9 +436,8 @@
     lane = lax.broadcasted_iota(jnp.int32, (length, LANES), 1)
     low = lane < HEAD_DIM
     first = lane % HEAD_DIM < HEAD_DIM // 2
-    for c in input_copies[2:]:
-        c.wait()
-    cos, sin = cos_ref[...], sin_ref[...]
+    local(tables, tables, in_sem.at[1]).wait()
+    cos, sin = tables[0], tables[1]
     causal = lax.broadcasted_iota(jnp.int32, (length, length), 0) >= lax.broadcasted_iota(
         jnp.int32, (length, length), 1
     )
@@ -462,21 +467,26 @@
     ]
 
     def attend():
-        for b, g, at in blocks:
-            kcut, cut = slice(b * LANES, (b + 1) * LANES), slice(at * LANES, (at + 1) * LANES)
-            keys = halves(rope(k_acc[:, kcut]))
-            values = halves(v_acc[:, kcut])
-            q = rope(q_acc[:, cut]).astype(BF16)
-            att = None
-            for side in range(2):
-                s = dot(q, keys[g][side], NT) * HEAD_DIM ** (-0.5)
-                s = jnp.where(causal, s, -jnp.inf)
-                e = jnp.exp(s - jnp.max(s, axis=1, keepdims=True))
-                p = (e / jnp.sum(e, axis=1, keepdims=True)).astype(BF16)
-                probs[2 * at + side] = p
-                a = dot(p, values[g][side])
-                att = a if att is None else att + a
-            att_own[:, cut] = att.astype(BF16)
+        for b in range(kv_cols // LANES):
+            kcut = slice(q_cols + b * LANES, q_cols + (b + 1) * LANES)
+            vcut = slice(kv_at + b * LANES, kv_at + (b + 1) * LANES)
+            keys = [jnp.concatenate(h, axis=0) for h in halves(rope(qkv_acc[:, kcut]))]
+            values = [jnp.concatenate(h, axis=0) for h in halves(qkv_acc[:, vcut])]
+            for of, g, at in blocks:
+                if of != b:
+                    continue
+                cut = slice(at * LANES, (at + 1) * LANES)
+                q = rope(qkv_acc[:, cut]).astype(BF16)
+                both = dot(q, keys[g], NT) * HEAD_DIM ** (-0.5)
+                weights = []
+                for side in range(2):
+                    s = jnp.where(causal, both[:, side * length : (side + 1) * length], -jnp.inf)
+                    e = jnp.exp(s - jnp.max(s, axis=1, keepdims=True))
+                    p = (e / jnp.sum(e, axis=1, keepdims=True)).astype(BF16)
+                    probs[2 * at + side] = p
+                    weights.append(p)
+                a = dot(jnp.concatenate(weights, axis=1), values[g])
+                att_own[:, cut] = a.astype(BF16)
 
     def grad_values():
         sums = {}
@@ -496,28 +506,28 @@
 
     def a_copy(d):
         return remote(
-            att_own, a_in.at[2 * (d - 1)], a_snd.at[d - 1], a_rcv.at[d - 1],
+            att_own, a_in.at[2 * (d - 1)], snd.at[0], a_rcv.at[d - 1],
             {"seq": device(d, core)},
         )
 
     def a_far():
         return remote(
-            att_own, ad_in.at[0], a_snd.at[far - 1], a_rcv.at[far - 1],
+            att_own, ad_in.at[0], snd.at[0], a_rcv.at[far - 1],
             {"seq": device(far, core)},
         )
 
     def a_beside():
-        return remote(att_own, ab_in, b_snd.at[tp], b_rcv.at[tp], {"seq": partner})
+        return remote(att_own, ab_in, snd.at[0], b_rcv.at[1], {"seq": partner})
 
     def a_pass(d):
         return remote(
-            a_in.at[2 * (d - 1)], a_in.at[2 * (d - 1) + 1], af_snd.at[d - 1],
+            a_in.at[2 * (d - 1)], a_in.at[2 * (d - 1) + 1], snd.at[0],
             af_rcv.at[d - 1], {"seq": partner},
         )
 
     def a_far_pass():
         return remote(
-            ad_in.at[0], ad_in.at[1], af_snd.at[far - 1], af_rcv.at[far - 1], {"seq": partner}
+            ad_in.at[0], ad_in.at[1], snd.at[0], af_rcv.at[far - 1], {"seq": partner}
         )
 
     def send_attended():
@@ -539,18 +549,18 @@
 
     def g_copy(d, other):
         return remote(
-            gv_own, g_in.at[2 * (d - 1) + other], g_snd.at[other, d - 1],
-            g_rcv.at[other, d - 1], {"seq": device(-d, (core + other) % 2)},
+            gv_own, g_in.at[2 * (d - 1) + other], snd.at[0],
+            g_rcv.at[d - 1], {"seq": device(-d, (core + other) % 2)},
         )
 
     def g_far(other):
         return remote(
-            gv_own, gd_in.at[other], g_snd.at[other, far - 1], g_rcv.at[other, far - 1],
+            gv_own, gd_in.at[other], snd.at[0], g_rcv.at[far - 1],
             {"seq": device(far, (core + other) % 2)},
         )
 
     def g_beside():
-        return remote(gv_own, gb_in, b_snd.at[tp + 1], b_rcv.at[tp + 1], {"seq": partner})
+        return remote(gv_own, gb_in, snd.at[0], b_rcv.at[2], {"seq": partner})
 
     def send_grads():
         @pl.when(low_chip)
@@ -576,8 +586,8 @@
         over[2 * d - 1] = two(att_own, a_in, 2 * (d - 1))
 
     def overlap_grads(d):
-        for other in range(2):
-            g_copy(d, other).wait_recv()
+        both = g_in.at[pl.ds(2 * (d - 1), 2)]
+        remote(both, both, snd.at[0], g_rcv.at[d - 1], {"seq": partner}).wait_recv()
         over[2 * d - 2] = two(gv_own, g_in, 2 * (d - 1))
 
     def overlap_far_attended():
@@ -589,8 +599,7 @@
     def overlap_far_grads():
         @pl.when(chip >= far)
         def _():
-            for other in range(2):
-                g_far(other).wait_recv()
+            remote(gd_in, gd_in, snd.at[0], g_rcv.at[far - 1], {"seq": partner}).wait_recv()
             over[ring - 2] = two(gv_own, gd_in, 0)
 
     def score(g, hop):
@@ -630,17 +639,20 @@
     for k in range(2, tp - 1):
         settle(0, k)
         arrivals(k, project_states)
+
+    each(0, ring - 2, chain)
     multiply_far()
-    each(0, ring - 2, chain)
     relay_down(1, 1, lower)
+    chain(ring - 2)
     for k in range(2, tp):
         relay(1, k)
-    chain(ring - 2)
     for k in range(max(2, tp - 1), tp):
         settle(0, k)
         arrivals(k, project_states)
+
     attend()
     send_attended()
+
     square(0, range(tp))
     for k in range(1, tp):
         settle(1, k)
@@ -696,10 +708,18 @@
     for k in range(1, tp):
         for which in range(2):
             for h in range(HALVES):
-                done_up = which * (k == col + 1) * (col >= mid) * (core == 0)
-                done_down = which * (k == tp - col) * (col < mid) * (core == 0)
-                pl.when(sends_up(k) & (done_up == 0))(lambda: up(which, k, h).wait_send())
-                pl.when(sends_down(k) & (done_down == 0))(lambda: down(which, k, h).wait_send())
+                if k == 1:
+                    pl.when(sends_up(k))(lambda: up(which, k, h).wait_send())
+                    pl.when(sends_down(k))(lambda: down(which, k, h).wait_send())
+                else:
+                    lasts_up, lasts_down = ends_up(which, k - 1), ends_down(which, k - 1)
+                    pl.when(sends_up(k) & jnp.logical_not(lasts_up))(
+                        lambda: up(which, k, h).wait_send()
+                    )
+                    pl.when(sends_down(k) & jnp.logical_not(lasts_down))(
+                        lambda: down(which, k, h).wait_send()
+                    )
+    pl.when((core == 1) & jnp.logical_not(edge))(last_relays)
 
     def drain_near(d):
         for c in (x_copy(d), c_copy(d), x_pass(d), c_pass(d), a_copy(d), a_pass(d)):
@@ -772,19 +792,13 @@
         in_specs=[hbm] * 8,
         out_specs=vmem,
         scratch_shapes=[
-            half(length, width),
-            half(length, width),
-            wide(length, LANES),
-            wide(length, LANES),
+            half(2, length, width),
+            wide(2, length, LANES),
             half(tp - 1, length, width),
             half(tp - 1, length, width),
-            half(tp, width, wq.shape[1]),
-            half(tp, width, kv),
-            half(tp, width, kv),
-            half(tp, wo.shape[0], width),
-            wide(length, wq.shape[1]),
-            wide(length, kv),
-            wide(length, kv),
+            half(tp * width, wq.shape[1] + 2 * kv),
+            half(wo.shape[0], tp * width),
+            wide(length, wq.shape[1] + 2 * kv),
             wide(length, wo.shape[0]),
             half(2 * near, length, width),
             half(2 * near, length, width),
@@ -807,25 +821,20 @@
             wide(ring - 1, length, 2 * length),
             wide(-(-n // 8) * 8, LANES),
             wide(tp * n, 1, lanes),
-            sem((4,)),
+            sem((2,)),
             pltpu.SemaphoreType.REGULAR,
-            sem((4 * tp,)),
-            sem((2, 2, tp - 1, HALVES)),
+            sem((2,)),
+            sem((1,)),
+            sem((HALVES,)),
             sem((2, tp - 1, HALVES)),
-            sem((3, far)),
-            sem((3, far)),
-            sem((3, far)),
-            sem((3, far)),
-            sem((tp + 2,)),
-            sem((tp + 2,)),
+            sem((2, near)),
+            sem((1,)),
+            sem((2, near)),
+            sem((1,)),
+            sem((3,)),
             sem((far,)),
             sem((far,)),
             sem((far,)),
-            sem((far,)),
-            sem((2, far)),
-            sem((2, far)),
-            sem((ring - 1,)),
-            sem((ring - 1,)),
             sem((ring - 1,)),
             sem((ring - 1,)),
             sem((ring - 1,)),

time: 35.3 us -> 34.3 us (0.972)
  Pallas kernels: 34.6 us -> 33.6 us
    pallas_call x1, Pallas kernels: 34.6 us -> 33.6 us  [on_device(): pl.pallas_call(functools.partial(kernel, n, tp), out_shape=pltpu.VMEM((1,...]
where the time goes in v5:
time: 34.3 us; the launch traced here: 34.1 us
  Pallas kernels  33.6 us (98%)
  local copies, waits for them, and re-layouts  0.51 us (1%)
    pallas_call x1, Pallas kernels, on_device(): pl.pallas_call(functools.partial(kernel, n, tp), out_shape=pltpu.VMEM((1,...  33.6 us

profile of v5, /device:TPU:0, one launch (start us, length us, event | category | flops | bytes accessed | tf_op | source)
XLA Modules:
  0.0 34.1 jit_solution(2611078410165119060)
XLA Ops:
  0.0 33.6 %ntk_gram.1 = f32[1,8]{1,0:T(1,128)S(1)} custom-call(bf16[128,512]{1,0:T(8,128)(2,1)} %bitcast.2, bf16[128,512]{1,0:T(8,128)(2,1)} %bitcast.3, f32[128,128]{1,0:T(8,128)} %constant.4.clone.cos_hbm, f32[128,128]{1,0:T(8,128)} %constant.5.clone.sin_hbm, bf16[2048,512]{1,0:T(8,128)(2,1)} %wq_hbm.1, bf16[2048,128]{1,0:T(8,128)(2,1)} %wk_hbm.1, ...), custom_call_target="tpu_custom_call" | custom-call | tf_op jit(solution)/shard_map/ntk_gram/pallas_call | solution.py:789
  33.6 0.5 %copy.10 = f32[1,8]{1,0:T(1,128)} copy(f32[1,8]{1,0:T(1,128)S(1)} %ntk_gram.1) | data formatting | bytes 64

commit v6 on v5

--- a/solution.py
+++ b/solution.py
@@ -60,12 +60,13 @@
     states_hbm, cot_hbm, cos_hbm, sin_hbm, wq_hbm, wk_hbm, wv_hbm, wo_hbm,
     out_ref,
     own, tables, xs, cs, wqkv, wob, qkv_acc, g_acc,
-    x_in, c_in, d_in, b_in, att_own, a_in, ad_in, ab_in, gv_own, g_in, gd_in, gb_in,
+    x_in, c_in, d_in, b_in, att, a_in, ad_in, gv, g_in, gd_in,
     probs, ad, rin, xin, full, near, over, sums, t2,
-    in_sem, clear_sem, w_sem, snd, last_snd, z_rcv, p_rcv, pd_rcv, f_rcv, fd_rcv, b_rcv,
-    a_rcv, af_rcv, g_rcv, r_rcv, s_rcv, o_rcv, r2_snd, r2_rcv,
+    in_sem, clear_sem, w_sem, snd, last_snd, z_rcv, p_rcv, pd_rcv, pair_rcv, b_rcv,
+    a_rcv, g_rcv, r_rcv, s_rcv, o_rcv, r2_snd, r2_rcv,
 ):
-    states_ref, cot_ref = own.at[0], own.at[1]
+    states_ref, cot_ref = own.at[0, 0], own.at[1, 0]
+    att_own, gv_own = att.at[0], gv.at[0]
     length, width = states_ref.shape
     q_cols = wq_hbm.shape[1]
     kv_cols = wk_hbm.shape[1]
@@ -73,7 +74,7 @@
     far = ring // 2
     mid = tp // 2
     hrows = length // HALVES
-    lanes = t2.shape[2]
+    lanes = t2.shape[2] // 2
     me = lax.axis_index("seq")
     col = lax.axis_index("tp")
     place = place_of(me, n)
@@ -100,8 +101,8 @@
 
     local = pltpu.make_async_copy
     input_copies = [
-        local(states_hbm, own.at[0], in_sem.at[0]),
-        local(cot_hbm, own.at[1], in_sem.at[0]),
+        local(states_hbm, states_ref, in_sem.at[0]),
+        local(cot_hbm, cot_ref, in_sem.at[0]),
         local(cos_hbm, tables.at[0], in_sem.at[1]),
         local(sin_hbm, tables.at[1], in_sem.at[1]),
     ]
@@ -123,7 +124,7 @@
     each(1, n, lambda o: pl.semaphore_signal(barrier, inc=1, device_id={"seq": (me + o) % n}))
     for c in input_copies:
         c.start()
-    local(own, own, in_sem.at[0]).wait()
+    local(own.at[0], own.at[0], in_sem.at[0]).wait()
     ends = (col == 0).astype(jnp.int32) + (col == last).astype(jnp.int32)
     pl.semaphore_wait(barrier, n + 1 - ends)
 
@@ -226,57 +227,37 @@
 
     def x_copy(d):
         return remote(
-            states_ref, x_in.at[2 * (d - 1)], snd.at[0], p_rcv.at[0, d - 1],
+            states_ref, x_in.at[d - 1], snd.at[0], p_rcv.at[0, d - 1],
             {"seq": device(-d, core)},
         )
 
     def c_copy(d):
         return remote(
-            cot_ref, c_in.at[2 * (d - 1)], snd.at[0], p_rcv.at[1, d - 1],
+            cot_ref, c_in.at[d - 1], snd.at[0], p_rcv.at[1, d - 1],
             {"seq": device(d, core)},
         )
 
     def far_copy(src):
         return remote(
-            src, d_in.at[0], snd.at[0], pd_rcv.at[0], {"seq": device(far, core)}
-        )
-
-    def x_pass(d):
-        return remote(
-            x_in.at[2 * (d - 1)], x_in.at[2 * (d - 1) + 1], snd.at[0],
-            f_rcv.at[0, d - 1], {"seq": partner},
-        )
-
-    def c_pass(d):
-        return remote(
-            c_in.at[2 * (d - 1)], c_in.at[2 * (d - 1) + 1], snd.at[0],
-            f_rcv.at[1, d - 1], {"seq": partner},
-        )
-
-    def far_pass():
-        return remote(
-            d_in.at[0], d_in.at[1], snd.at[0], fd_rcv.at[0], {"seq": partner}
+            src, d_in, snd.at[0], pd_rcv.at[0], {"seq": device(far, core)}
+        )
+
+    def pair_copy(which):
+        return remote(
+            own.at[which, 0], own.at[which, 1], snd.at[0], pair_rcv.at[0], {"seq": partner}
         )
 
     def start_near(d):
         x_copy(d).start()
         c_copy(d).start()
 
+    for which in range(2):
+        pair_copy(which).start()
     each(1, far, start_near)
     pl.when(low_chip)(lambda: far_copy(states_ref).start())
     pl.when(chip >= far)(lambda: far_copy(cot_ref).start())
     for c in weight_copies:
         c.start()
-
-    def pass_near(d):
-        x_copy(d).wait_recv()
-        x_pass(d).start()
-        c_copy(d).wait_recv()
-        c_pass(d).start()
-
-    def pass_far():
-        far_copy(states_ref).wait_recv()
-        far_pass().start()
 
     def own_block(which, slot):
         return inputs[which] if slot == 0 else held[which].at[slot - 1]
@@ -391,15 +372,17 @@
                     {"tp": (col + tp - 1) % tp},
                 ).wait_send()
 
-    def send_totals():
-        inside = jnp.logical_not(edge)
-        pl.when(inside & (core == 1))(lambda: pl.semaphore_wait(clear_sem, 1))
-        pl.when(central)(lambda: each(0, ring - 1, lambda g: outer(g, lambda c: c.start())))
-
-        @pl.when(inside & (core == 0))
+    def total_out(g):
+        total(g)
+        pl.when(central)(lambda: outer(g, lambda c: c.start()))
+
+    def clear_links():
+        @pl.when(jnp.logical_not(edge) & (core == 0))
         def _():
             last_relays()
             pl.semaphore_signal(clear_sem, inc=1, device_id={"seq": partner})
+
+        pl.when(jnp.logical_not(edge) & (core == 1))(lambda: pl.semaphore_wait(clear_sem, 1))
 
     def totals_here(g):
         @pl.when(jnp.logical_not(central))
@@ -407,9 +390,8 @@
             waits_on(full, o_rcv, g)
             pl.when(jnp.logical_not(edge))(lambda: outer(g, lambda c: c.start()))
 
-    def two(own, buf, at):
-        both = buf[pl.ds(at, 2)].reshape(2 * length, buf.shape[2])
-        return dot(own[...], both, NT)
+    def two(pair, other):
+        return dot(other[...], pair[...].reshape(2 * length, pair.shape[2]), NT)
 
     def put(g, tiles):
         ad[2 * g] = tiles[:, :length].astype(BF16)
@@ -417,21 +399,15 @@
         publish(g)
 
     def multiply_near(d):
-        x_pass(d).wait_recv()
-        put(2 * d - 2, two(states_ref, x_in, 2 * (d - 1)))
-        c_pass(d).wait_recv()
-        put(2 * d - 1, two(cot_ref, c_in, 2 * (d - 1)))
+        x_copy(d).wait_recv()
+        put(2 * d - 2, two(own.at[0], x_in.at[d - 1]))
+        c_copy(d).wait_recv()
+        put(2 * d - 1, two(own.at[1], c_in.at[d - 1]))
 
     def multiply_far():
-        far_pass().wait_recv()
-
-        @pl.when(low_chip)
-        def _():
-            put(ring - 2, two(cot_ref, d_in, 0))
-
-        @pl.when(chip >= far)
-        def _():
-            put(ring - 2, two(states_ref, d_in, 0))
+        far_copy(states_ref).wait_recv()
+        pl.when(low_chip)(lambda: put(ring - 2, two(own.at[1], d_in)))
+        pl.when(chip >= far)(lambda: put(ring - 2, two(own.at[0], d_in)))
 
     lane = lax.broadcasted_iota(jnp.int32, (length, LANES), 1)
     low = lane < HEAD_DIM
@@ -506,107 +482,71 @@
 
     def a_copy(d):
         return remote(
-            att_own, a_in.at[2 * (d - 1)], snd.at[0], a_rcv.at[d - 1],
-            {"seq": device(d, core)},
+            att_own, a_in.at[d - 1], snd.at[0], a_rcv.at[d - 1], {"seq": device(d, core)}
         )
 
     def a_far():
         return remote(
-            att_own, ad_in.at[0], snd.at[0], a_rcv.at[far - 1],
-            {"seq": device(far, core)},
+            att_own, ad_in, snd.at[0], a_rcv.at[far - 1], {"seq": device(far, core)}
         )
 
     def a_beside():
-        return remote(att_own, ab_in, snd.at[0], b_rcv.at[1], {"seq": partner})
-
-    def a_pass(d):
-        return remote(
-            a_in.at[2 * (d - 1)], a_in.at[2 * (d - 1) + 1], snd.at[0],
-            af_rcv.at[d - 1], {"seq": partner},
-        )
-
-    def a_far_pass():
-        return remote(
-            ad_in.at[0], ad_in.at[1], snd.at[0], af_rcv.at[far - 1], {"seq": partner}
-        )
+        return remote(att_own, att.at[1], snd.at[0], b_rcv.at[1], {"seq": partner})
 
     def send_attended():
         each(1, far, lambda d: a_copy(d).start())
         pl.when(chip >= far)(lambda: a_far().start())
-        pl.when(core == 0)(lambda: a_beside().start())
-
-    def pass_attended():
-        def one(d):
-            a_copy(d).wait_recv()
-            a_pass(d).start()
-
-        each(1, far, one)
-
+        a_beside().start()
+
+    def g_copy(d):
+        return remote(
+            gv_own, g_in.at[d - 1], snd.at[0], g_rcv.at[d - 1], {"seq": device(-d, core)}
+        )
+
+    def g_far():
+        return remote(
+            gv_own, gd_in, snd.at[0], g_rcv.at[far - 1], {"seq": device(far, core)}
+        )
+
+    def g_beside():
+        return remote(gv_own, gv.at[1], snd.at[0], b_rcv.at[2], {"seq": partner})
+
+    def send_grads():
+        pl.when(low_chip)(lambda: g_far().start())
+        each(1, far, lambda d: g_copy(d).start())
+        g_beside().start()
+
+    lane_at = lax.broadcasted_iota(jnp.int32, (1, lanes), 1)
+
+    def weigh(row, source, d, b):
+        at = pl.ds(source, 1)
+        sums[row, at, :] = sums[row, at, :] + jnp.sum(d * b, axis=0, keepdims=True)
+
+    def overlap_attended(d):
+        a_copy(d).wait_recv()
+        over[2 * d - 1] = two(att, a_in.at[d - 1])
+
+    def overlap_grads(d):
+        g_copy(d).wait_recv()
+        over[2 * d - 2] = two(gv, g_in.at[d - 1])
+
+    def overlap_far_attended():
         @pl.when(low_chip)
         def _():
             a_far().wait_recv()
-            a_far_pass().start()
-
-    def g_copy(d, other):
-        return remote(
-            gv_own, g_in.at[2 * (d - 1) + other], snd.at[0],
-            g_rcv.at[d - 1], {"seq": device(-d, (core + other) % 2)},
-        )
-
-    def g_far(other):
-        return remote(
-            gv_own, gd_in.at[other], snd.at[0], g_rcv.at[far - 1],
-            {"seq": device(far, (core + other) % 2)},
-        )
-
-    def g_beside():
-        return remote(gv_own, gb_in, snd.at[0], b_rcv.at[2], {"seq": partner})
-
-    def send_grads():
-        @pl.when(low_chip)
-        def _():
-            for other in range(2):
-                g_far(other).start()
-
-        def one(d):
-            for other in range(2):
-                g_copy(d, other).start()
-
-        each(1, far, one)
-        pl.when(core == 1)(lambda: g_beside().start())
-
-    lane_at = lax.broadcasted_iota(jnp.int32, (1, lanes), 1)
-
-    def weigh(source, d, b):
-        at = pl.ds(source, 1)
-        sums[at, :] = sums[at, :] + jnp.sum(d * b, axis=0, keepdims=True)
-
-    def overlap_attended(d):
-        a_pass(d).wait_recv()
-        over[2 * d - 1] = two(att_own, a_in, 2 * (d - 1))
-
-    def overlap_grads(d):
-        both = g_in.at[pl.ds(2 * (d - 1), 2)]
-        remote(both, both, snd.at[0], g_rcv.at[d - 1], {"seq": partner}).wait_recv()
-        over[2 * d - 2] = two(gv_own, g_in, 2 * (d - 1))
-
-    def overlap_far_attended():
-        @pl.when(low_chip)
-        def _():
-            a_far_pass().wait_recv()
-            over[ring - 2] = two(att_own, ad_in, 0)
+            over[ring - 2] = two(att, ad_in)
 
     def overlap_far_grads():
         @pl.when(chip >= far)
         def _():
-            remote(gd_in, gd_in, snd.at[0], g_rcv.at[far - 1], {"seq": partner}).wait_recv()
-            over[ring - 2] = two(gv_own, gd_in, 0)
+            g_far().wait_recv()
+            over[ring - 2] = two(gv, gd_in)
 
     def score(g, hop):
-        for other in range(2):
+        for row in range(2):
             weigh(
-                device(hop, (core + other) % 2), full[2 * g + other].astype(F32),
-                over[g, :, other * length : (other + 1) * length],
+                row, device(hop, core), full[2 * g + row].astype(F32),
+                over[g, :, row * length : (row + 1) * length],
             )
 
     def score_near(d):
@@ -619,7 +559,7 @@
     project_states(0)
     relay_first()
     follow(1)
-    each(1, far, pass_near)
+    remote(own.at[0], own.at[0], snd.at[0], pair_rcv.at[0], {"seq": partner}).wait_recv()
     settle(0, 1)
     arrivals(1, project_states)
     if tp > 2:
@@ -635,7 +575,6 @@
         follow(k)
     project_cot(0)
     relay_up(1, 1, upper)
-    pass_far()
     for k in range(2, tp - 1):
         settle(0, k)
         arrivals(k, project_states)
@@ -643,6 +582,12 @@
     each(0, ring - 2, chain)
     multiply_far()
     relay_down(1, 1, lower)
+
+    @pl.when(jnp.logical_not(edge))
+    def _():
+        attend()
+        send_attended()
+
     chain(ring - 2)
     for k in range(2, tp):
         relay(1, k)
@@ -650,8 +595,10 @@
         settle(0, k)
         arrivals(k, project_states)
 
-    attend()
-    send_attended()
+    @pl.when(edge)
+    def _():
+        attend()
+        send_attended()
 
     square(0, range(tp))
     for k in range(1, tp):
@@ -659,19 +606,18 @@
         arrivals(k, project_cot)
     grad_values()
     send_grads()
-    each(0, ring - 1, total)
-    send_totals()
+    pl.when(core == 0)(lambda: each(0, ring - 1, total_out))
+    pl.when(core == 1)(lambda: each(0, ring - 1, total))
+    clear_links()
+    pl.when((core == 1) & central)(
+        lambda: each(0, ring - 1, lambda g: outer(g, lambda c: c.start()))
+    )
     square(1, range(tp))
     multiply_beside(0)
-    pass_attended()
+    a_beside().wait_recv()
     sums[...] = jnp.zeros_like(sums)
-    weigh(me, near[1], dot(att_own[...], att_own[...], NT))
-    weigh(me, near[0], dot(gv_own[...], gv_own[...], NT))
-
-    @pl.when(core == 0)
-    def _():
-        g_beside().wait_recv()
-        weigh(partner, near[2], dot(gv_own[...], gb_in[...], NT))
+    weigh(0, me, near[1], dot(att_own[...], att_own[...], NT))
+    weigh(0, me, near[0], dot(gv_own[...], gv_own[...], NT))
 
     each(1, far, overlap_attended)
     overlap_far_attended()
@@ -679,8 +625,13 @@
 
     @pl.when(core == 1)
     def _():
-        a_beside().wait_recv()
-        weigh(partner, near[2], dot(att_own[...], ab_in[...], NT))
+        weigh(0, partner, near[2], dot(att_own[...], att[1], NT))
+
+    g_beside().wait_recv()
+
+    @pl.when(core == 0)
+    def _():
+        weigh(0, partner, near[2], dot(gv_own[...], gv[1], NT))
 
     each(1, far, overlap_grads)
     overlap_far_grads()
@@ -690,10 +641,11 @@
 
     row_at = lax.broadcasted_iota(jnp.int32, (n, lanes), 0)
     spot_at = lax.broadcasted_iota(jnp.int32, (n, lanes), 1)
-    pairs = jnp.sum(sums[...], axis=1, keepdims=True)[:n]
-    t2[col * n + me] = jnp.sum(
-        jnp.where(row_at == spot_at, pairs, 0.0), axis=0, keepdims=True
-    )
+    for row in range(2):
+        pairs = jnp.sum(sums[row], axis=1, keepdims=True)[:n]
+        t2[col * n + me, :, row * lanes : (row + 1) * lanes] = jnp.sum(
+            jnp.where(row_at == spot_at, pairs, 0.0), axis=0, keepdims=True
+        )
 
     def send_scalars(plane, o):
         mine = t2.at[col * n + me]
@@ -722,25 +674,17 @@
     pl.when((core == 1) & jnp.logical_not(edge))(last_relays)
 
     def drain_near(d):
-        for c in (x_copy(d), c_copy(d), x_pass(d), c_pass(d), a_copy(d), a_pass(d)):
+        for c in (x_copy(d), c_copy(d), a_copy(d), g_copy(d)):
             c.wait_send()
-        for other in range(2):
-            g_copy(d, other).wait_send()
 
     each(1, far, drain_near)
     far_copy(states_ref).wait_send()
-    far_pass().wait_send()
+    for c in (pair_copy(0), pair_copy(1), a_beside(), g_beside()):
+        c.wait_send()
     for slot in range(tp):
         beside(0, slot).wait_send()
     pl.when(chip >= far)(lambda: a_far().wait_send())
-    pl.when(core == 0)(lambda: a_beside().wait_send())
-    pl.when(core == 1)(lambda: g_beside().wait_send())
-
-    @pl.when(low_chip)
-    def _():
-        a_far_pass().wait_send()
-        for other in range(2):
-            g_far(other).wait_send()
+    pl.when(low_chip)(lambda: g_far().wait_send())
 
     def drain_sums(g):
         inner(g, lambda c: c.wait_send())
@@ -750,9 +694,12 @@
     others = t2.at[pl.ds(0, n * tp - 1)]
     everyone = remote(others, others, r2_snd.at[0], r2_rcv.at[0], {"seq": partner})
     everyone.wait_recv()
-    table = t2[pl.ds(0, n)].reshape(n, lanes)
+    both = t2[pl.ds(0, n)].reshape(n, 2 * lanes)
     for q in range(1, tp):
-        table = table + t2[pl.ds(q * n, n)].reshape(n, lanes)
+        both = both + t2[pl.ds(q * n, n)].reshape(n, 2 * lanes)
+    aside = both[:, lanes:]
+    aside = jnp.where(row_at % 2 == 0, pltpu.roll(aside, n - 1, 0), pltpu.roll(aside, 1, 0))
+    table = both[:, :lanes] + aside
     rank, spot = row_at, spot_at
     eye = rank == spot
     column = jnp.sum(jnp.where(spot == me, table, 0.0), axis=1, keepdims=True)
@@ -792,7 +739,7 @@
         in_specs=[hbm] * 8,
         out_specs=vmem,
         scratch_shapes=[
-            half(2, length, width),
+            half(2, 2, length, width),
             wide(2, length, LANES),
             half(tp - 1, length, width),
             half(tp - 1, length, width),
@@ -800,17 +747,15 @@
             half(wo.shape[0], tp * width),
             wide(length, wq.shape[1] + 2 * kv),
             wide(length, wo.shape[0]),
-            half(2 * near, length, width),
-            half(2 * near, length, width),
+            half(near, length, width),
+            half(near, length, width),
+            half(length, width),
+            half(tp, length, width),
             half(2, length, width),
-            half(tp, length, width),
+            half(near, length, width),
             half(length, width),
-            half(2 * near, length, width),
-            half(2, length, width),
-            half(length, width),
-            half(length, kv),
-            half(2 * near, length, kv),
             half(2, length, kv),
+            half(near, length, kv),
             half(length, kv),
             half(width // HEAD_DIM, length, length),
             half(tiles, length, length),
@@ -819,8 +764,8 @@
             half(tiles, length, length),
             wide(3, length, length),
             wide(ring - 1, length, 2 * length),
-            wide(-(-n // 8) * 8, LANES),
-            wide(tp * n, 1, lanes),
+            wide(2, -(-n // 8) * 8, LANES),
+            wide(tp * n, 1, 2 * lanes),
             sem((2,)),
             pltpu.SemaphoreType.REGULAR,
             sem((2,)),
@@ -829,10 +774,8 @@
             sem((2, tp - 1, HALVES)),
             sem((2, near)),
             sem((1,)),
-            sem((2, near)),
             sem((1,)),
             sem((3,)),
-            sem((far,)),
             sem((far,)),
             sem((far,)),
             sem((ring - 1,)),

time: 34.3 us -> 34.2 us (level)
  no operation moved by 1% of the time
where the time goes in v6:
time: 34.2 us; the launch traced here: 34.1 us
  Pallas kernels  33.5 us (98%)
  local copies, waits for them, and re-layouts  0.51 us (1%)
    pallas_call x1, Pallas kernels, on_device(): pl.pallas_call(functools.partial(kernel, n, tp), out_shape=pltpu.VMEM((1,...  33.5 us

profile of v6, /device:TPU:0, one launch (start us, length us, event | category | flops | bytes accessed | tf_op | source)
XLA Modules:
  0.0 34.1 jit_solution(6295275687009887460)
XLA Ops:
  0.0 33.5 %ntk_gram.1 = f32[1,8]{1,0:T(1,128)S(1)} custom-call(bf16[128,512]{1,0:T(8,128)(2,1)} %bitcast.2, bf16[128,512]{1,0:T(8,128)(2,1)} %bitcast.3, f32[128,128]{1,0:T(8,128)} %constant.4.clone.cos_hbm, f32[128,128]{1,0:T(8,128)} %constant.5.clone.sin_hbm, bf16[2048,512]{1,0:T(8,128)(2,1)} %wq_hbm.1, bf16[2048,128]{1,0:T(8,128)(2,1)} %wk_hbm.1, ...), custom_call_target="tpu_custom_call" | custom-call | tf_op jit(solution)/shard_map/ntk_gram/pallas_call | solution.py:736
  33.5 0.5 %copy.10 = f32[1,8]{1,0:T(1,128)} copy(f32[1,8]{1,0:T(1,128)S(1)} %ntk_gram.1) | data formatting | bytes 64

commit v7 on v6

--- a/solution.py
+++ b/solution.py
@@ -379,7 +379,6 @@
     def clear_links():
         @pl.when(jnp.logical_not(edge) & (core == 0))
         def _():
-            last_relays()
             pl.semaphore_signal(clear_sem, inc=1, device_id={"seq": partner})
 
         pl.when(jnp.logical_not(edge) & (core == 1))(lambda: pl.semaphore_wait(clear_sem, 1))
@@ -671,7 +670,7 @@
                     pl.when(sends_down(k) & jnp.logical_not(lasts_down))(
                         lambda: down(which, k, h).wait_send()
                     )
-    pl.when((core == 1) & jnp.logical_not(edge))(last_relays)
+    pl.when(jnp.logical_not(edge))(last_relays)
 
     def drain_near(d):
         for c in (x_copy(d), c_copy(d), a_copy(d), g_copy(d)):

time: 34.2 us -> 34.2 us (level)
  no operation moved by 1% of the time
where the time goes in v7:
time: 34.2 us; the launch traced here: 34.1 us
  Pallas kernels  33.5 us (98%)
  local copies, waits for them, and re-layouts  0.51 us (1%)
    pallas_call x1, Pallas kernels, on_device(): pl.pallas_call(functools.partial(kernel, n, tp), out_shape=pltpu.VMEM((1,...  33.5 us

profile of v7, /device:TPU:0, one launch (start us, length us, event | category | flops | bytes accessed | tf_op | source)
XLA Modules:
  0.0 34.1 jit_solution(12234295592137430885)
XLA Ops:
  0.0 33.5 %ntk_gram.1 = f32[1,8]{1,0:T(1,128)S(1)} custom-call(bf16[128,512]{1,0:T(8,128)(2,1)} %bitcast.2, bf16[128,512]{1,0:T(8,128)(2,1)} %bitcast.3, f32[128,128]{1,0:T(8,128)} %constant.4.clone.cos_hbm, f32[128,128]{1,0:T(8,128)} %constant.5.clone.sin_hbm, bf16[2048,512]{1,0:T(8,128)(2,1)} %wq_hbm.1, bf16[2048,128]{1,0:T(8,128)(2,1)} %wk_hbm.1, ...), custom_call_target="tpu_custom_call" | custom-call | tf_op jit(solution)/shard_map/ntk_gram/pallas_call | solution.py:735
  33.5 0.5 %copy.10 = f32[1,8]{1,0:T(1,128)} copy(f32[1,8]{1,0:T(1,128)S(1)} %ntk_gram.1) | data formatting | bytes 64
